TPU v7x, 32 devices: a whole 2x2x4 slice. The times are simulated.
32 devices in a mesh: wide: 4 (over z), tp: 2 (over y), rep: 4 (over x, core).
Axes of the slice: x: 2, y: 2, z: 4, core: 2. Of those that a mesh axis runs over, the one named last changes fastest.
Arguments:
- activations: bfloat16 [32768, 8192], P('rep', 'wide'), may hold values from -6 to 6
- value_grads: bfloat16 [32768, 1024], P('rep', 'tp'), may hold values from -24 to 24
- seq_lengths: int32 [32], P('rep'), may hold values from 128 to 1024
- master: float32 [8192, 1024], P(('wide', 'rep'), 'tp'), may hold values from -0.0625 to 0.0625
- first_moment: float32 [8192, 1024], P(('wide', 'rep'), 'tp'), may hold values from -3 to 3
- second_moment: float32 [8192, 1024], P(('wide', 'rep'), 'tp'), may hold values from 0.05 to 2
- hidden: bfloat16 [4, 64, 8192], P(None, ('wide', 'rep')), may hold values from -6 to 6
- queries: bfloat16 [4, 64, 8192], P(None, ('wide', 'rep'), 'tp'), may hold values from -200 to 200
- new_keys: bfloat16 [4, 64, 1024], P(None, ('wide', 'rep'), 'tp'), may hold values from -6 to 6
- cache_keys: bfloat16 [64, 256, 1024], P(('wide', 'rep'), None, 'tp'), may hold values from -6 to 6
- cache_values: bfloat16 [64, 256, 1024], P(('wide', 'rep'), None, 'tp'), may hold values from -6 to 6
- cache_lengths: int32 [64], P(('wide', 'rep')), may hold values from 2 to 256
Outputs:
- new_master: float32 [8192, 1024], P(('wide', 'rep'), 'tp')
- new_first: float32 [8192, 1024], P(('wide', 'rep'), 'tp')
- new_second: float32 [8192, 1024], P(('wide', 'rep'), 'tp')
- new_values: bfloat16 [4, 64, 1024], P(None, ('wide', 'rep'), 'tp')
- attended: bfloat16 [4, 64, 8192], P(None, ('wide', 'rep'), 'tp')
All inputs are finite; a program needn't handle non-finite values.
Results may differ from a plain program's by a relative error of at most 0.012.
Values may be sent and summed in bfloat16 or wider, within the bound.
No kernel may reach another device: no remote copies, remote signals or barrier semaphores. Data moves between devices by JAX's collectives and lax.ppermute only.
A program may use at most 128 MiB of HBM per device.

v0:
```python
import functools

import jax
import jax.numpy as jnp
from jax import lax
from jax.experimental import pallas as pl
from jax.experimental.pallas import tpu as pltpu
from jax.sharding import PartitionSpec as P


HEADS = 64
KV_HEADS = 8
HEAD = 128
QUANT = 128


beta_one = 0.9
beta_two = 0.95
learn_rate = 0.001
weight_decay = 0.1
epsilon = 1e-08
steps_done = 10.0
quant_top = 448.0
scale_epsilon = 1e-06


def quantize(weights):
    row_count, col_count = weights.shape
    tiled = weights.reshape(row_count, col_count // QUANT, QUANT)
    largest = jnp.max(jnp.abs(tiled), axis=2)
    scales = ((largest + scale_epsilon) / quant_top).astype(jnp.bfloat16)
    quantized = (tiled / scales.astype(jnp.float32)[:, :, None]).astype(jnp.bfloat16)
    return (quantized.reshape(row_count, col_count), scales)


def dequantize(quantized, scales):
    row_count, col_count = quantized.shape
    tiled = quantized.astype(jnp.float32).reshape(row_count, col_count // QUANT, QUANT)
    return (tiled * scales.astype(jnp.float32)[:, :, None]).reshape(row_count, col_count)


def on_device_plain(
    activations,
    value_grads,
    seq_lengths,
    master,
    first_moment,
    second_moment,
    hidden,
    queries,
    new_keys,
    cache_keys,
    cache_values,
    cache_lengths,
):
    seq_count = seq_lengths.shape[0]
    token_count, col_count = value_grads.shape
    seq_span = token_count // seq_count
    position = jnp.arange(seq_span, dtype=jnp.int32)
    lengths = seq_lengths.astype(jnp.float32)
    token_weight = jnp.where(position[None, :] < seq_lengths[:, None], 1.0 / lengths[:, None], 0.0)
    weighted = (
        value_grads.astype(jnp.float32).reshape(seq_count, seq_span, col_count)
        * token_weight[:, :, None]
    ).astype(jnp.bfloat16)
    weighted = weighted.reshape(token_count, col_count)
    gradient = lax.psum_scatter(
        lax.dot_general(
            activations, weighted, (((0,), (0,)), ((), ())), preferred_element_type=jnp.float32
        ),
        "rep",
        scatter_dimension=0,
        tiled=True,
    )
    new_first = beta_one * first_moment + (1.0 - beta_one) * gradient
    new_second = beta_two * second_moment + (1.0 - beta_two) * gradient * gradient
    corrected_first = new_first / (1.0 - beta_one**steps_done)
    corrected_second = new_second / (1.0 - beta_two**steps_done)
    new_master = master - learn_rate * (
        corrected_first / (jnp.sqrt(corrected_second) + epsilon) + weight_decay * master
    )
    quantized, scales = quantize(new_master)
    step_count, row_local, width = hidden.shape
    score_scale = HEAD ** (-0.5)
    group = HEADS // KV_HEADS
    kv_local = col_count // HEAD
    query = queries.reshape(step_count, row_local, kv_local, group, HEAD)
    keys_cache = cache_keys.reshape(row_local, cache_keys.shape[1], kv_local, HEAD)
    values_cache = cache_values.reshape(row_local, cache_values.shape[1], kv_local, HEAD)
    keys_new = new_keys.reshape(step_count, row_local, kv_local, HEAD)
    slots = jnp.arange(cache_keys.shape[1], dtype=jnp.int32)
    cache_live = slots[None, :] < cache_lengths[:, None]
    scores_cache = (
        jnp.einsum("sbgrd,bjgd->sbgrj", query, keys_cache, preferred_element_type=jnp.float32)
        * score_scale
    )
    scores_cache = jnp.where(cache_live[None, :, None, None, :], scores_cache, -jnp.inf)
    scores_new = (
        jnp.einsum("sbgrd,tbgd->sbgrt", query, keys_new, preferred_element_type=jnp.float32)
        * score_scale
    )
    moments = jnp.arange(step_count, dtype=jnp.int32)
    earlier = moments[None, :] <= moments[:, None]
    scores_new = jnp.where(earlier[:, None, None, None, :], scores_new, -jnp.inf)
    highest = jnp.maximum(jnp.max(scores_cache, axis=4), jnp.max(scores_new, axis=4))
    exp_cache = jnp.exp(scores_cache - highest[..., None])
    exp_new = jnp.exp(scores_new - highest[..., None])
    totals = jnp.sum(exp_cache, axis=4) + jnp.sum(exp_new, axis=4)
    probs_cache = (exp_cache / totals[..., None]).astype(jnp.bfloat16)
    probs_new = (exp_new / totals[..., None]).astype(jnp.bfloat16)
    mixed_cache = jnp.einsum(
        "sbgrj,bjgd->sbgrd", probs_cache, values_cache, preferred_element_type=jnp.float32
    )
    wide_count = lax.axis_size("wide")
    rep_count = lax.axis_size("rep")
    block_rows = width // (wide_count * rep_count)
    arranged = hidden.reshape(step_count, row_local, wide_count, rep_count, block_rows)
    swapped = lax.all_to_all(arranged, "rep", split_axis=3, concat_axis=1, tiled=True)
    group_rows = rep_count * row_local
    flat_group = swapped.reshape(step_count * group_rows, wide_count * block_rows).astype(
        jnp.float32
    )
    quant_rows = lax.all_gather(quantized, "wide", axis=0, tiled=True)
    scale_rows = lax.all_gather(scales, "wide", axis=0, tiled=True)
    weight_rows = dequantize(quant_rows, scale_rows)
    partial_value = jnp.dot(
        flat_group, weight_rows, precision=lax.Precision.HIGHEST, preferred_element_type=jnp.float32
    )
    partial_value = partial_value.reshape(step_count, group_rows, col_count)
    projected = lax.psum_scatter(partial_value, "rep", scatter_dimension=1, tiled=True)
    new_values = projected.astype(jnp.bfloat16)
    values_new = new_values.reshape(step_count, row_local, kv_local, HEAD)
    mixed = mixed_cache + jnp.einsum(
        "sbgrt,tbgd->sbgrd", probs_new, values_new, preferred_element_type=jnp.float32
    )
    attended = mixed.astype(jnp.bfloat16).reshape(step_count, row_local, kv_local * group * HEAD)
    return (new_master, new_first, new_second, new_values, attended)


TOKEN_BLOCK = 256
STEP_BLOCKS = 2
BUFFERS = 4
PAD = 4 * STEP_BLOCKS


def live_blocks(lengths, block_of, span, limit_of=None, length_of=None, begin=None):
    count = jnp.int32(0)
    per_seq = span // TOKEN_BLOCK

    def note(place, block, limit, length):
        block_of[place] = block
        if limit_of is not None:
            limit_of[place] = limit
            length_of[place] = length

    for seq in range(lengths.shape[0]):
        length = lengths[seq]
        for part in range(per_seq):
            note(count, seq * per_seq + part, length - part * TOKEN_BLOCK, length)
            count = count + jnp.where(length > part * TOKEN_BLOCK, 1, 0)
        if begin is not None and seq % STEP_BLOCKS == STEP_BLOCKS - 1 and seq // STEP_BLOCKS < BUFFERS - 1:
            begin(jnp.int32(seq // STEP_BLOCKS))
    for pad in range(PAD):
        note(count + pad, 0, 0, 1)
    return lax.div(count + STEP_BLOCKS - 1, STEP_BLOCKS)


def start_acts(acts, buf, sem, block_of, step, column, parts):
    width = buf.shape[1]
    for part in range(parts):
        first = pl.multiple_of(block_of[step * STEP_BLOCKS + part] * TOKEN_BLOCK, TOKEN_BLOCK)
        pltpu.make_async_copy(
            acts.at[pl.ds(first, TOKEN_BLOCK), pl.ds(column, width)],
            buf.at[part * TOKEN_BLOCK : (part + 1) * TOKEN_BLOCK],
            sem,
        ).start()


def wait_acts(acts, buf, sem):
    rows, cols = buf.shape
    pltpu.make_async_copy(acts.at[pl.ds(0, rows), pl.ds(0, cols)], buf, sem).wait()


def product(left, right):
    return jnp.dot(left, right, preferred_element_type=jnp.float32)


def first_kernel(
    span,
    width,
    wide_count,
    rep_count,
    lengths,
    acts,
    grads,
    hidden,
    ours,
    theirs,
    weighted,
    pieces,
    ahead,
    block_of,
    limit_of,
    length_of,
    acts_buf,
    grads_buf,
    even,
    odd,
    acc,
    loaded,
    flat,
    acts_sem,
    grads_sem,
    hidden_sem,
    ahead_sem,
):
    rep = lax.axis_index("rep")
    here = lax.axis_index("wide")
    core = lax.rem(rep, 2)
    chip = lax.div(rep, 2)
    column = pl.multiple_of((1 - chip) * 2 * width, 2 * width)
    next_column = pl.multiple_of((chip * 2 + 1 - core) * width, width)
    step_rows = STEP_BLOCKS * TOKEN_BLOCK
    cols = grads.shape[1]
    fetch = pltpu.make_async_copy(hidden, loaded, hidden_sem)
    fetch.start()

    def start(step):
        slot = lax.rem(step, BUFFERS)
        start_acts(grads, grads_buf.at[slot], grads_sem.at[slot], block_of, step, 0, STEP_BLOCKS)
        start_acts(acts, acts_buf.at[slot], acts_sem.at[slot], block_of, step, column, STEP_BLOCKS)

    def turn(step, target):
        slot = lax.rem(step, BUFFERS)
        for part in range(STEP_BLOCKS):
            entry = step * STEP_BLOCKS + part
            rows = slice(part * TOKEN_BLOCK, (part + 1) * TOKEN_BLOCK)
            value = grads_buf[slot, rows, :].astype(jnp.float32)
            length = jnp.full((1, cols), length_of[entry], jnp.int32).astype(jnp.float32)
            position = lax.broadcasted_iota(jnp.int32, value.shape, 0)
            scaled = jnp.where(position < limit_of[entry], value * (1.0 / length), 0.0)
            turned = scaled.astype(jnp.bfloat16).T
            target[:, rows] = turned
            place = pl.multiple_of(step * step_rows + part * TOKEN_BLOCK, TOKEN_BLOCK)
            weighted[:, pl.ds(place, TOKEN_BLOCK)] = turned

    steps = live_blocks(lengths, block_of, span, limit_of, length_of, start)
    start_acts(acts, ahead, ahead_sem, block_of, 0, next_column, 4 * STEP_BLOCKS)
    acc[...] = jnp.zeros_like(acc)
    fetch.wait()
    count, rows, _ = loaded.shape
    for step in range(count):
        flat[step * rows : (step + 1) * rows, :] = loaded[step].astype(jnp.float32)
    for dc in range(2):
        for dx in range(2):
            for dz in range(wide_count):
                place = (here ^ dz) * rep_count + (chip ^ dx) * 2 + (core ^ dc)
                begin = pl.multiple_of(place * width, width)
                pieces[dc * 2 + dx, dz] = flat[:, pl.ds(begin, width)].astype(jnp.bfloat16)

    wait_acts(grads, grads_buf.at[0], grads_sem.at[0])
    turn(jnp.int32(0), even)

    def phase(step, source, target):
        @pl.when(step + BUFFERS - 1 < steps)
        def _():
            start(step + BUFFERS - 1)

        @pl.when(step + 1 < steps)
        def _():
            slot = lax.rem(step + 1, BUFFERS)
            wait_acts(grads, grads_buf.at[slot], grads_sem.at[slot])

        slot = lax.rem(step, BUFFERS)
        wait_acts(acts, acts_buf.at[slot], acts_sem.at[slot])
        turn(step + 1, target)
        acc[...] += product(source[...], acts_buf[slot])

    def body(pair, carry):
        phase(2 * pair, even, odd)
        phase(2 * pair + 1, odd, even)
        return carry

    lax.fori_loop(0, lax.div(steps, 2), body, 0)

    @pl.when(lax.rem(steps, 2) == 1)
    def _():
        slot = lax.rem(steps - 1, BUFFERS)
        wait_acts(acts, acts_buf.at[slot], acts_sem.at[slot])
        acc[...] += product(even[...], acts_buf[slot])

    split(acc, core, ours, theirs)
    wait_acts(acts, ahead, ahead_sem)


def split(acc, core, ours, theirs):
    width = ours.shape[1]
    ours[...] = acc[:, pl.ds(pl.multiple_of(core * width, width), width)]
    theirs[...] = acc[:, pl.ds(pl.multiple_of((1 - core) * width, width), width)].astype(jnp.bfloat16)


def own_kernel(
    span,
    width,
    mine,
    lengths,
    acts,
    weighted,
    loaded,
    order,
    *refs,
):
    del order
    if mine:
        out, block_of, acts_buf, acc, acts_sem = refs
    else:
        out, ahead, block_of, acts_buf, acc, acts_sem, ahead_sem = refs
    rep = lax.axis_index("rep")
    core = lax.rem(rep, 2)
    first_column = lax.div(rep, 2) * 2 * width
    my_column = pl.multiple_of(first_column + core * width, width)
    column = my_column if mine else pl.multiple_of(first_column + (1 - core) * width, width)
    steps = live_blocks(lengths, block_of, span)
    trips = lax.div(steps, 4)
    rest = lax.rem(steps, 4)
    step_rows = STEP_BLOCKS * TOKEN_BLOCK
    trip_rows = 4 * step_rows
    slots = acts_buf.shape[0]
    held = trips + jnp.where(rest > 0, 1, 0)

    def start(trip):
        slot = lax.rem(trip, slots)
        start_acts(
            acts, acts_buf.at[slot], acts_sem.at[slot], block_of, 4 * trip, column, 4 * STEP_BLOCKS
        )

    for early in range(1, slots):
        @pl.when(early < held)
        def _():
            start(jnp.int32(early))

    if not mine:
        start_acts(acts, ahead, ahead_sem, block_of, 0, my_column, 4 * STEP_BLOCKS)
    acc[...] = product(weighted[:, :trip_rows], loaded[...])

    def body(trip, carry):
        @pl.when(trip + slots - 1 < held)
        def _():
            start(trip + slots - 1)

        slot = lax.rem(trip, slots)
        wait_acts(acts, acts_buf.at[slot], acts_sem.at[slot])
        lanes = pl.ds(pl.multiple_of(trip * trip_rows, trip_rows), trip_rows)
        acc[...] += product(weighted[:, lanes], acts_buf[slot])
        return carry

    lax.fori_loop(1, trips, body, 0)
    slot = lax.rem(trips, slots)
    begin = trips * trip_rows

    @pl.when(rest > 0)
    def _():
        wait_acts(acts, acts_buf.at[slot], acts_sem.at[slot])

    @pl.when(rest > 1)
    def _():
        lanes = pl.ds(pl.multiple_of(begin, trip_rows), 2 * step_rows)
        acc[...] += product(weighted[:, lanes], acts_buf[slot, : 2 * step_rows])

    @pl.when(lax.rem(rest, 2) == 1)
    def _():
        skipped = pl.multiple_of((rest - 1) * step_rows, 2 * step_rows)
        lanes = pl.ds(pl.multiple_of(begin + skipped, 2 * step_rows), step_rows)
        acc[...] += product(weighted[:, lanes], acts_buf[slot, pl.ds(skipped, step_rows)])

    out[...] = acc[...].astype(out.dtype)
    if not mine:
        wait_acts(acts, ahead, ahead_sem)


def update_kernel(
    own, from_core, from_chip, master, first, second, kept, sent,
    new_master, new_first, new_second, partial_kept, partial_sent,
):
    for tile in range(own.shape[0] // QUANT):
        part = slice(tile * QUANT, (tile + 1) * QUANT)
        total = own[part] + from_core[part].astype(jnp.float32) + from_chip[part].astype(jnp.float32)
        gradient = total.T
        moved_first = beta_one * first[:, part] + (1.0 - beta_one) * gradient
        moved_second = beta_two * second[:, part] + (1.0 - beta_two) * gradient * gradient
        corrected_first = moved_first * (learn_rate / (1.0 - beta_one**steps_done))
        corrected_second = moved_second * (1.0 / (1.0 - beta_two**steps_done))
        moved = master[:, part] * (1.0 - learn_rate * weight_decay) - corrected_first / (
            jnp.sqrt(corrected_second) + epsilon
        )
        new_first[:, part] = moved_first
        new_second[:, part] = moved_second
        new_master[:, part] = moved
        largest = jnp.max(jnp.abs(moved), axis=1, keepdims=True)
        scales = ((largest + scale_epsilon) / quant_top).astype(jnp.bfloat16).astype(jnp.float32)
        quantized = (moved * (1.0 / scales)).astype(jnp.bfloat16).astype(jnp.float32)
        used = quantized * scales
        high = used.astype(jnp.bfloat16)
        low = (used - high.astype(jnp.float32)).astype(jnp.bfloat16)
        partial_sent[:, part] = (product(sent[...], high) + product(sent[...], low)).astype(jnp.bfloat16)
        partial_kept[:, part] = product(kept[...], high) + product(kept[...], low)


def attention_kernel(
    lengths, queries, new_keys, cache_keys, cache_values, master, first, second,
    mixed, late, master_out, first_out, second_out, flat, keys, sems,
):
    writes = [
        pltpu.make_async_copy(source, target, sems.at[place])
        for place, (source, target) in enumerate(
            ((master, master_out), (first, first_out), (second, second_out))
        )
    ]
    for write in writes:
        write.start()
    steps, seqs, _ = queries.shape
    slots = cache_keys.shape[1]
    kv_local = new_keys.shape[2] // HEAD
    group = HEADS // KV_HEADS
    lines = steps * seqs
    for step in range(steps):
        flat[step * seqs : (step + 1) * seqs, :] = queries[step].astype(jnp.float32)
        keys[step * seqs : (step + 1) * seqs, :] = new_keys[step].astype(jnp.float32)
    rows = group * lines

    def index(shape, axis):
        return lax.broadcasted_iota(jnp.int32, shape, axis)

    wide_shape = (rows, slots)
    seq_of = lax.rem(index(wide_shape, 0), seqs)
    limit = jnp.zeros(wide_shape, jnp.int32)
    for seq in range(seqs):
        limit = jnp.where(seq_of == seq, lengths[seq], limit)
    live = index(wide_shape, 1) < limit
    late_shape = (rows, lines)
    late_row = index(late_shape, 0)
    late_col = index(late_shape, 1)
    allowed = (lax.rem(late_row, seqs) == lax.rem(late_col, seqs)) & (
        lax.div(late_col, seqs) <= lax.rem(lax.div(late_row, seqs), steps)
    )
    score_scale = HEAD ** (-0.5)
    across = (((1,), (1,)), ((), ()))
    for head in range(kv_local):
        lanes = slice(head * HEAD, (head + 1) * HEAD)
        query = jnp.concatenate(
            [
                flat[:, (head * group + part) * HEAD : (head * group + part + 1) * HEAD]
                for part in range(group)
            ],
            axis=0,
        ).astype(jnp.bfloat16)
        scores = jnp.zeros(wide_shape, jnp.float32)
        for seq in range(seqs):
            one = lax.dot_general(
                query, cache_keys[seq, :, lanes], across, preferred_element_type=jnp.float32
            )
            scores = jnp.where(seq_of == seq, one, scores)
        scores = jnp.where(live, scores * score_scale, -jnp.inf)
        scores_new = (
            lax.dot_general(
                query, keys[:, lanes].astype(jnp.bfloat16), across, preferred_element_type=jnp.float32
            )
            * score_scale
        )
        scores_new = jnp.where(allowed, scores_new, -jnp.inf)
        highest = jnp.maximum(
            jnp.max(scores, axis=1, keepdims=True), jnp.max(scores_new, axis=1, keepdims=True)
        )
        exp_cache = jnp.exp(scores - highest)
        exp_new = jnp.exp(scores_new - highest)
        totals = jnp.sum(exp_cache, axis=1, keepdims=True) + jnp.sum(exp_new, axis=1, keepdims=True)
        probs = exp_cache / totals
        late[head] = (exp_new / totals).astype(jnp.bfloat16)
        result = jnp.zeros((rows, HEAD), jnp.float32)
        for seq in range(seqs):
            mine = jnp.where(seq_of == seq, probs, 0.0).astype(jnp.bfloat16)
            result = result + jnp.dot(
                mine, cache_values[seq, :, lanes], preferred_element_type=jnp.float32
            )
        mixed[head] = result
    for write in writes:
        write.wait()


def finish_kernel(steps, seqs, *refs):
    mixed, late, own = refs[:3]
    arrived = refs[3:-3]
    new_values, attended, flat = refs[-3:]
    total = own[...]
    for block in arrived:
        total = total + block[...].astype(jnp.float32)
    values = total.astype(jnp.bfloat16)
    wide_values = values.astype(jnp.float32)
    lines = steps * seqs
    kv_local, rows, _ = mixed.shape
    group = rows // lines
    for head in range(kv_local):
        lanes = slice(head * HEAD, (head + 1) * HEAD)
        result = mixed[head] + jnp.dot(late[head], values[:, lanes], preferred_element_type=jnp.float32)
        for part in range(group):
            flat[:, (head * group + part) * HEAD : (head * group + part + 1) * HEAD] = result[
                part * lines : (part + 1) * lines, :
            ]
    for step in range(steps):
        new_values[step] = wide_values[step * seqs : (step + 1) * seqs, :].astype(jnp.bfloat16)
        attended[step] = flat[step * seqs : (step + 1) * seqs, :].astype(jnp.bfloat16)


HBM = pl.BlockSpec(memory_space=pltpu.HBM)
VMEM = pl.BlockSpec(memory_space=pltpu.VMEM)
SMEM = pl.BlockSpec(memory_space=pltpu.SMEM)
PARAMS = pltpu.CompilerParams(vmem_limit_bytes=24 * 1024 * 1024)


def on_device(
    activations,
    value_grads,
    seq_lengths,
    master,
    first_moment,
    second_moment,
    hidden,
    queries,
    new_keys,
    cache_keys,
    cache_values,
    cache_lengths,
):
    shape = jax.ShapeDtypeStruct
    bf16, f32 = jnp.bfloat16, jnp.float32
    wide_count = lax.axis_size("wide")
    rep_count = lax.axis_size("rep")
    tokens, cols = value_grads.shape
    seqs = seq_lengths.shape[0]
    span = tokens // seqs
    step_count, row_local, _ = hidden.shape
    lines = step_count * row_local
    width = master.shape[0]
    blocks = tokens // TOKEN_BLOCK + PAD
    step_rows = STEP_BLOCKS * TOKEN_BLOCK

    core_pairs = [(i, i ^ 1) for i in range(rep_count)]
    chip_pairs = [(i, i ^ 2) for i in range(rep_count)]

    table = pltpu.SMEM((blocks,), jnp.int32)

    def buffers(rows, columns):
        return pltpu.VMEM((BUFFERS, rows, columns), bf16)

    sems = pltpu.SemaphoreType.DMA((BUFFERS,))
    ours, for_core, weighted, pieces, ahead = pl.pallas_call(
        functools.partial(first_kernel, span, width, wide_count, rep_count),
        out_shape=(
            shape((cols, width), f32),
            shape((cols, width), bf16),
            pltpu.VMEM((cols, tokens + step_rows), bf16),
            shape((4, wide_count, lines, width), bf16),
            pltpu.VMEM((4 * step_rows, width), bf16),
        ),
        in_specs=[SMEM, HBM, HBM, HBM],
        out_specs=(VMEM,) * 5,
        scratch_shapes=[
            table,
            table,
            table,
            buffers(step_rows, 2 * width),
            buffers(step_rows, cols),
            pltpu.VMEM((cols, step_rows), bf16),
            pltpu.VMEM((cols, step_rows), bf16),
            pltpu.VMEM((cols, 2 * width), f32),
            pltpu.VMEM(hidden.shape, bf16),
            pltpu.VMEM((lines, hidden.shape[2]), f32),
            sems,
            sems,
            pltpu.SemaphoreType.DMA,
            pltpu.SemaphoreType.DMA,
        ],
        compiler_params=PARAMS,
        name="first_chunk",
    )(seq_lengths, activations, in_hbm(value_grads), in_hbm(hidden))
    core_part = lax.ppermute(for_core, "rep", core_pairs)
    both_pairs = [(i, i ^ 3) for i in range(rep_count)]
    moved = jnp.stack(
        [
            pieces[0],
            lax.ppermute(pieces[1], "rep", chip_pairs),
            lax.ppermute(pieces[2], "rep", core_pairs),
            lax.ppermute(pieces[3], "rep", both_pairs),
        ]
    )

    for_chip = (ours + core_part.astype(f32)).astype(bf16)
    chip_part = lax.ppermute(for_chip, "rep", chip_pairs)

    def own_call(mine, ahead, order, out_shape):
        return pl.pallas_call(
            functools.partial(own_kernel, span, width, mine),
            out_shape=out_shape,
            in_specs=[SMEM, HBM, VMEM, VMEM, HBM],
            out_specs=(VMEM,) * len(out_shape),
            scratch_shapes=[
                table,
                pltpu.VMEM((BUFFERS - 1, 4 * step_rows, width), bf16),
                pltpu.VMEM((cols, width), f32),
                pltpu.SemaphoreType.DMA((BUFFERS - 1,)),
            ]
            + [pltpu.SemaphoreType.DMA] * (not mine),
            compiler_params=PARAMS,
            name="own_chunk" if mine else "near_chunk",
        )(seq_lengths, activations, weighted, ahead, order)

    for_core, ahead = own_call(
        False, ahead, for_chip, (shape((cols, width), bf16), pltpu.VMEM((4 * step_rows, width), bf16))
    )
    core_part = lax.ppermute(for_core, "rep", core_pairs)
    pieces = [moved[:, 0]]
    for dz in range(1, wide_count):
        pairs = [(i, i ^ dz) for i in range(wide_count)]
        pieces.append(lax.ppermute(moved[:, dz], "wide", pairs))
    moved = jnp.stack(pieces, axis=1)
    group_rows = 2 * wide_count * lines
    hidden_kept = moved[:2].reshape(group_rows, width)
    hidden_sent = moved[2:].reshape(group_rows, width)

    (own_part,) = own_call(True, ahead, for_core, (shape((cols, width), f32),))
    new_master, new_first, new_second, kept, sent = pl.pallas_call(
        update_kernel,
        out_shape=(pltpu.VMEM((width, cols), f32),) * 3
        + (shape((group_rows, cols), f32), shape((group_rows, cols), bf16)),
        in_specs=[VMEM] * 8,
        out_specs=(VMEM,) * 5,
        compiler_params=PARAMS,
        name="update",
    )(own_part, core_part, chip_part, master, first_moment, second_moment, hidden_kept, hidden_sent)
    summed = kept + lax.ppermute(sent, "rep", core_pairs).astype(f32)
    half = wide_count * lines
    summed = summed[:half] + lax.ppermute(summed[half:].astype(bf16), "rep", chip_pairs).astype(f32)
    arrived = []
    for place in range(1, wide_count):
        pairs = [(i, i ^ place) for i in range(wide_count)]
        arrived.append(
            lax.ppermute(summed[place * lines : (place + 1) * lines].astype(bf16), "wide", pairs)
        )
    kv_local = cols // HEAD
    rows = (HEADS // KV_HEADS) * lines
    mixed, late, new_master, new_first, new_second = pl.pallas_call(
        attention_kernel,
        out_shape=(
            shape((kv_local, rows, HEAD), f32),
            shape((kv_local, rows, lines), bf16),
            *(pltpu.HBM((width, cols), f32),) * 3,
        ),
        in_specs=[SMEM] + [VMEM] * 7,
        out_specs=(VMEM, VMEM, HBM, HBM, HBM),
        scratch_shapes=[
            pltpu.VMEM((lines, queries.shape[2]), f32),
            pltpu.VMEM((lines, cols), f32),
            pltpu.SemaphoreType.DMA((3,)),
        ],
        compiler_params=PARAMS,
        name="cache_attention",
    )(cache_lengths, queries, new_keys, cache_keys, cache_values, new_master, new_first, new_second)
    new_values, attended = pl.pallas_call(
        functools.partial(finish_kernel, step_count, row_local),
        out_shape=(shape(new_keys.shape, bf16), shape(queries.shape, bf16)),
        in_specs=[VMEM] * (3 + len(arrived)),
        out_specs=(VMEM, VMEM),
        scratch_shapes=[pltpu.VMEM((lines, queries.shape[2]), f32)],
        compiler_params=PARAMS,
        name="finish",
    )(mixed, late, summed[:lines], *arrived)
    return (new_master, new_first, new_second, new_values, attended)


def in_hbm(value):
    return pltpu.with_memory_space_constraint(value, pltpu.HBM)


def dispatch(*args):
    _, value_grads, seq_lengths, master, _, _, hidden = args[:7]
    lines = hidden.shape[0] * hidden.shape[1]
    wide_count = lax.axis_size("wide")
    fits = (
        lax.axis_size("rep") == 4
        and wide_count & (wide_count - 1) == 0
        and master.shape[0] % 128 == 0
        and master.shape[1] % QUANT == 0
        and (value_grads.shape[0] // seq_lengths.shape[0]) % TOKEN_BLOCK == 0
        and lines == 16
        and seq_lengths.shape[0] >= BUFFERS * STEP_BLOCKS
    )
    if not fits:
        return on_device_plain(*args)
    return on_device(*args)


def solution(mesh):
    in_specs = (
        P("rep", "wide"),
        P("rep", "tp"),
        P("rep"),
        P(("wide", "rep"), "tp"),
        P(("wide", "rep"), "tp"),
        P(("wide", "rep"), "tp"),
        P(None, ("wide", "rep"), None),
        P(None, ("wide", "rep"), "tp"),
        P(None, ("wide", "rep"), "tp"),
        P(("wide", "rep"), None, "tp"),
        P(("wide", "rep"), None, "tp"),
        P(("wide", "rep")),
    )
    out_specs = (
        P(("wide", "rep"), "tp"),
        P(("wide", "rep"), "tp"),
        P(("wide", "rep"), "tp"),
        P(None, ("wide", "rep"), "tp"),
        P(None, ("wide", "rep"), "tp"),
    )
    return jax.shard_map(
        dispatch, mesh=mesh, in_specs=in_specs, out_specs=out_specs, check_vma=False
    )
```

profile of v0, /device:TPU:0, one launch (start us, length us, event | category | flops | bytes accessed | tf_op | source)
XLA Modules:
  0.0 62.9 jit_solution(2871092820185017226)
XLA Ops:
  0.6 0.6 %copy-done.7 = s32[8]{0:T(128)S(1)} copy-done((s32[8]{0:T(128)S(1)}, s32[8]{0:T(128)}, u32[]{:S(2)}) %copy-start.7) | copy-done | bytes 56
  1.3 11.9 %first_chunk.1 = (f32[512,512]{1,0:T(8,128)S(1)}, bf16[512,512]{1,0:T(8,128)(2,1)S(1)}, bf16[512,8704]{1,0:T(8,128)(2,1)S(1)}, bf16[4,4,16,512]{3,2,1,0:T(8,128)(2,1)S(1)}, bf16[2048,512]{1,0:T(8,128)(2,1)S(1)}) custom-call(s32[8]{0:T(128)S(1)} %copy-done.7, bf16[8192,2048]{1,0:T(8,128)(2,1)} %acts.5, bf16[8192,512]{1,0:T(8,128)(2,1)} %grads.1, ...), custom_call_target="tpu_custom_call" | custom-call | tf_op jit(solution)/shard_map/first_chunk/pallas_call | solution.py:556
  13.2 0.6 collective-permute-start
  13.8 4.0 %collective-permute-start.5 = (bf16[4,16,512]{2,1,0:T(8,128)(2,1)S(1)}, bf16[4,16,512]{2,1,0:T(8,128)(2,1)S(1)}, u32[]{:S(2)}, u32[]{:S(2)}) collective-permute-start(bf16[4,16,512]{2,1,0:T(8,128)(2,1)S(1)} %get-tuple-element.52), channel_id=1, source_target_pairs={{0,3},{1,2},{2,1},{3,0},{4,7},{5,6},{6,5},{7,4},{8,11},{9,10},{10,... | collective-permute-start | bytes 196616 | tf_op jit(solution)/shard_map/ppermute | solution.py:593
  17.8 0.0 collective-permute-start.4
  17.8 0.5 collective-permute-start.3
  18.2 2.0 %collective-permute-done.5 = bf16[4,16,512]{2,1,0:T(8,128)(2,1)S(1)} collective-permute-done((bf16[4,16,512]{2,1,0:T(8,128)(2,1)S(1)}, bf16[4,16,512]{2,1,0:T(8,128)(2,1)S(1)}, u32[]{:S(2)}, u32[]{:S(2)}) %collective-permute-start.5) | collective-permute-done | bytes 65568 | tf_op jit(solution)/shard_map/ppermute | solution.py:593
  20.3 2.0 %collective-permute-done.3 = bf16[4,16,512]{2,1,0:T(8,128)(2,1)S(1)} collective-permute-done((bf16[4,16,512]{2,1,0:T(8,128)(2,1)S(1)}, bf16[4,16,512]{2,1,0:T(8,128)(2,1)S(1)}, u32[]{:S(2)}, u32[]{:S(2)}) %collective-permute-start.3) | collective-permute-done | bytes 65568 | tf_op jit(solution)/shard_map/ppermute | solution.py:591
  22.3 0.2 add_convert_fusion.order
  22.5 1.3 %collective-permute-start.2 = (bf16[512,512]{1,0:T(8,128)(2,1)S(1)}, bf16[512,512]{1,0:T(8,128)(2,1)S(1)}, u32[]{:S(2)}, u32[]{:S(2)}) collective-permute-start(bf16[512,512]{1,0:T(8,128)(2,1)S(1)} %add_convert_fusion.order), channel_id=1, source_target_pairs={{0,2},{1,3},{2,0},{3,1},{4,6},{5,7},{6,4},{7,5},{8,10},{9,11},{10,... | collective-permute-start | bytes 1572872 | tf_op jit(solution)/shard_map/ppermute | solution.py:598
  23.7 5.6 %near_chunk.1 = (bf16[512,512]{1,0:T(8,128)(2,1)S(1)}, bf16[2048,512]{1,0:T(8,128)(2,1)S(1)}) custom-call(s32[8]{0:T(128)S(1)} %copy-done.7, bf16[8192,2048]{1,0:T(8,128)(2,1)} %acts.5, bf16[512,8704]{1,0:T(8,128)(2,1)S(1)} %get-tuple-element.24.weighted, bf16[2048,512]{1,0:T(8,128)(2,1)S(1)} %get-tuple-element.25.loaded, ...), custom_call_target="tpu_custom_call" | custom-call | tf_op jit(solution)/shard_map/near_chunk/pallas_call | solution.py:601
  29.4 0.1 collective-permute-start.1
  29.5 1.6 %collective-permute-start.6 = (bf16[4,16,512]{2,1,0:T(8,128)(2,1)S(1)}, bf16[4,16,512]{2,1,0:T(8,128)(2,1)S(1)}, u32[]{:S(2)}, u32[]{:S(2)}) collective-permute-start(bf16[4,16,512]{2,1,0:T(8,128)(2,1)S(1)} %get-tuple-element.48), channel_id=1, source_target_pairs={{0,8},{8,0},{16,24},{24,16},{1,9},{9,1},{17,25},{25,17},{2,10},{10... | collective-permute-start | bytes 196616 | tf_op jit(solution)/shard_map/ppermute | solution.py:624
  31.2 2.5 %collective-permute-start.8 = (bf16[4,16,512]{2,1,0:T(8,128)(2,1)S(1)}, bf16[4,16,512]{2,1,0:T(8,128)(2,1)S(1)}, u32[]{:S(2)}, u32[]{:S(2)}) collective-permute-start(bf16[4,16,512]{2,1,0:T(8,128)(2,1)S(1)} %get-tuple-element.49), channel_id=1, source_target_pairs={{0,24},{8,16},{16,8},{24,0},{1,25},{9,17},{17,9},{25,1},{2,26},{10... | collective-permute-start | bytes 196616 | tf_op jit(solution)/shard_map/ppermute | solution.py:624
  33.6 0.1 collective-permute-start.7
  33.7 0.3 collective-permute-done.6
  34.1 3.9 %collective-permute-done.8 = bf16[4,16,512]{2,1,0:T(8,128)(2,1)S(1)} collective-permute-done((bf16[4,16,512]{2,1,0:T(8,128)(2,1)S(1)}, bf16[4,16,512]{2,1,0:T(8,128)(2,1)S(1)}, u32[]{:S(2)}, u32[]{:S(2)}) %collective-permute-start.8) | collective-permute-done | bytes 65568 | tf_op jit(solution)/shard_map/ppermute | solution.py:624
  37.9 2.5 %collective-permute-done.7 = bf16[4,16,512]{2,1,0:T(8,128)(2,1)S(1)} collective-permute-done((bf16[4,16,512]{2,1,0:T(8,128)(2,1)S(1)}, bf16[4,16,512]{2,1,0:T(8,128)(2,1)S(1)}, u32[]{:S(2)}, u32[]{:S(2)}) %collective-permute-start.7) | collective-permute-done | bytes 65568 | tf_op jit(solution)/shard_map/ppermute | solution.py:624
  40.5 0.0 copy-start.1
  40.6 0.0 copy-start.2
  40.6 0.0 copy-start.4
  40.6 5.7 %own_chunk.1.own = f32[512,512]{1,0:T(8,128)S(1)} custom-call(s32[8]{0:T(128)S(1)} %copy-done.7, bf16[8192,2048]{1,0:T(8,128)(2,1)} %acts.5, bf16[512,8704]{1,0:T(8,128)(2,1)S(1)} %get-tuple-element.24.weighted, bf16[2048,512]{1,0:T(8,128)(2,1)S(1)} %get-tuple-element.28.loaded, bf16[512,512]{1,0:T(8,128)(2,1)S(1)} %get-tuple-element.29.order), custom_call_target="tpu_custom_call" | custom-call | tf_op jit(solution)/shard_map/own_chunk/pallas_call | solution.py:601
  46.4 2.0 %update.1 = (f32[512,512]{1,0:T(8,128)S(1)}, f32[512,512]{1,0:T(8,128)S(1)}, f32[512,512]{1,0:T(8,128)S(1)}, f32[128,512]{1,0:T(8,128)S(1)}, bf16[128,512]{1,0:T(8,128)(2,1)S(1)}) custom-call(f32[512,512]{1,0:T(8,128)S(1)} %own_chunk.1.own, bf16[512,512]{1,0:T(8,128)(2,1)S(1)} %collective-permute-done.1.from_core, ...), custom_call_target="tpu_custom_call" | custom-call | tf_op jit(solution)/shard_map/update/pallas_call | solution.py:631
  48.4 0.2 collective-permute-start.9
  48.6 1.3 %collective-permute-done.9 = bf16[128,512]{1,0:T(8,128)(2,1)S(1)} collective-permute-done((bf16[128,512]{1,0:T(8,128)(2,1)S(1)}, bf16[128,512]{1,0:T(8,128)(2,1)S(1)}, u32[]{:S(2)}, u32[]{:S(2)}) %collective-permute-start.9) | collective-permute-done | bytes 131104 | tf_op jit(solution)/shard_map/ppermute | solution.py:640
  49.9 2.3 %collective-permute-start.10 = (bf16[64,512]{1,0:T(8,128)(2,1)S(1)}, bf16[64,512]{1,0:T(8,128)(2,1)S(1)}, u32[]{:S(2)}, u32[]{:S(2)}) collective-permute-start(bf16[64,512]{1,0:T(8,128)(2,1)S(1)} %slice.89), channel_id=1, source_target_pairs={{0,2},{1,3},{2,0},{3,1},{4,6},{5,7},{6,4},{7,5},{8,10},{9,11},{10,... | collective-permute-start | bytes 196616 | tf_op jit(solution)/shard_map/ppermute | solution.py:642
  52.2 2.4 %collective-permute-done.10 = bf16[64,512]{1,0:T(8,128)(2,1)S(1)} collective-permute-done((bf16[64,512]{1,0:T(8,128)(2,1)S(1)}, bf16[64,512]{1,0:T(8,128)(2,1)S(1)}, u32[]{:S(2)}, u32[]{:S(2)}) %collective-permute-start.10) | collective-permute-done | bytes 65568 | tf_op jit(solution)/shard_map/ppermute | solution.py:642
  54.6 2.8 %collective-permute-start.13 = (bf16[16,512]{1,0:T(8,128)(2,1)S(1)}, bf16[16,512]{1,0:T(8,128)(2,1)S(1)}, u32[]{:S(2)}, u32[]{:S(2)}) collective-permute-start(bf16[16,512]{1,0:T(8,128)(2,1)S(1)} %get-tuple-element.55), channel_id=1, source_target_pairs={{0,24},{8,16},{16,8},{24,0},{1,25},{9,17},{17,9},{25,1},{2,26},{10... | collective-permute-start | bytes 49160 | tf_op jit(solution)/shard_map/ppermute | solution.py:647
  57.4 1.7 %collective-permute-start.11 = (bf16[16,512]{1,0:T(8,128)(2,1)S(1)}, bf16[16,512]{1,0:T(8,128)(2,1)S(1)}, u32[]{:S(2)}, u32[]{:S(2)}) collective-permute-start(bf16[16,512]{1,0:T(8,128)(2,1)S(1)} %get-tuple-element.57), channel_id=1, source_target_pairs={{0,8},{8,0},{16,24},{24,16},{1,9},{9,1},{17,25},{25,17},{2,10},{10... | collective-permute-start | bytes 49160 | tf_op jit(solution)/shard_map/ppermute | solution.py:647
  59.1 2.5 %cache_attention.1 = (f32[4,128,128]{2,1,0:T(8,128)S(1)}, bf16[4,128,16]{2,1,0:T(8,128)(2,1)S(1)}, f32[512,512]{1,0:T(8,128)}, f32[512,512]{1,0:T(8,128)}, f32[512,512]{1,0:T(8,128)}) custom-call(s32[4]{0:T(128)S(1)} %copy-done.8, bf16[4,4,4096]{2,1,0:T(4,128)(2,1)S(1)} %copy-done.5, bf16[4,4,512]{2,1,0:T(4,128)(2,1)S(1)} %copy-done.6, ...), custom_call_target="tpu_custom_call" | custom-call | tf_op jit(solution)/shard_map/cache_attention/pallas_call | solution.py:651
  61.7 0.3 collective-permute-done.12.refs_4_
  62.0 0.8 %finish.1 = (bf16[4,4,512]{2,1,0:T(4,128)(2,1)}, bf16[4,4,4096]{2,1,0:T(4,128)(2,1)}) custom-call(f32[4,128,128]{2,1,0:T(8,128)S(1)} %get-tuple-element.37.refs_0_, bf16[4,128,16]{2,1,0:T(8,128)(2,1)S(1)} %get-tuple-element.38.refs_1_, f32[16,512]{1,0:T(8,128)S(1)} %slice.76.refs_2_, bf16[16,512]{1,0:T(8,128)(2,1)S(1)} %collective-permute-done.11.refs_3_, ...), custom_call_target="tpu_custom_call" | custom-call | tf_op jit(solution)/shard_map/finish/pallas_call | solution.py:668
  (33 shorter events, 0.3 us)
Async XLA Ops:
  0.6 0.7 %copy-start.7 = (s32[8]{0:T(128)S(1)}, s32[8]{0:T(128)}, u32[]{:S(2)}) copy-start(s32[8]{0:T(128)} %lengths.6) | copy-start | bytes 100
  13.2 9.1 %collective-permute-start = (bf16[512,512]{1,0:T(8,128)(2,1)S(1)}, bf16[512,512]{1,0:T(8,128)(2,1)S(1)}, u32[]{:S(2)}, u32[]{:S(2)}) collective-permute-start(bf16[512,512]{1,0:T(8,128)(2,1)S(1)} %get-tuple-element.27), channel_id=1, source_target_pairs={{0,1},{1,0},{2,3},{3,2},{4,5},{5,4},{6,7},{7,6},{8,9},{9,8},{10,11... | collective-permute-start | bytes 1572872 | tf_op jit(solution)/shard_map/ppermute | solution.py:586
  13.8 6.5 %collective-permute-start.5 = (bf16[4,16,512]{2,1,0:T(8,128)(2,1)S(1)}, bf16[4,16,512]{2,1,0:T(8,128)(2,1)S(1)}, u32[]{:S(2)}, u32[]{:S(2)}) collective-permute-start(bf16[4,16,512]{2,1,0:T(8,128)(2,1)S(1)} %get-tuple-element.52), channel_id=1, source_target_pairs={{0,3},{1,2},{2,1},{3,0},{4,7},{5,6},{6,5},{7,4},{8,11},{9,10},{10,... | collective-permute-start | bytes 196616 | tf_op jit(solution)/shard_map/ppermute | solution.py:593
  17.8 2.5 %collective-permute-start.4 = (bf16[4,16,512]{2,1,0:T(8,128)(2,1)S(1)}, bf16[4,16,512]{2,1,0:T(8,128)(2,1)S(1)}, u32[]{:S(2)}, u32[]{:S(2)}) collective-permute-start(bf16[4,16,512]{2,1,0:T(8,128)(2,1)S(1)} %get-tuple-element.53), channel_id=1, source_target_pairs={{0,1},{1,0},{2,3},{3,2},{4,5},{5,4},{6,7},{7,6},{8,9},{9,8},{10,11... | collective-permute-start | bytes 196616 | tf_op jit(solution)/shard_map/ppermute | solution.py:592
  17.8 4.5 %collective-permute-start.3 = (bf16[4,16,512]{2,1,0:T(8,128)(2,1)S(1)}, bf16[4,16,512]{2,1,0:T(8,128)(2,1)S(1)}, u32[]{:S(2)}, u32[]{:S(2)}) collective-permute-start(bf16[4,16,512]{2,1,0:T(8,128)(2,1)S(1)} %get-tuple-element.54), channel_id=1, source_target_pairs={{0,2},{1,3},{2,0},{3,1},{4,6},{5,7},{6,4},{7,5},{8,10},{9,11},{10,... | collective-permute-start | bytes 196616 | tf_op jit(solution)/shard_map/ppermute | solution.py:591
  22.5 23.9 %collective-permute-start.2 = (bf16[512,512]{1,0:T(8,128)(2,1)S(1)}, bf16[512,512]{1,0:T(8,128)(2,1)S(1)}, u32[]{:S(2)}, u32[]{:S(2)}) collective-permute-start(bf16[512,512]{1,0:T(8,128)(2,1)S(1)} %add_convert_fusion.order), channel_id=1, source_target_pairs={{0,2},{1,3},{2,0},{3,1},{4,6},{5,7},{6,4},{7,5},{8,10},{9,11},{10,... | collective-permute-start | bytes 1572872 | tf_op jit(solution)/shard_map/ppermute | solution.py:598
  29.4 16.9 %collective-permute-start.1 = (bf16[512,512]{1,0:T(8,128)(2,1)S(1)}, bf16[512,512]{1,0:T(8,128)(2,1)S(1)}, u32[]{:S(2)}, u32[]{:S(2)}) collective-permute-start(bf16[512,512]{1,0:T(8,128)(2,1)S(1)} %get-tuple-element.29.order), channel_id=1, source_target_pairs={{0,1},{1,0},{2,3},{3,2},{4,5},{5,4},{6,7},{7,6},{8,9},{9,8},{10,11... | collective-permute-start | bytes 1572872 | tf_op jit(solution)/shard_map/ppermute | solution.py:620
  29.5 4.6 %collective-permute-start.6 = (bf16[4,16,512]{2,1,0:T(8,128)(2,1)S(1)}, bf16[4,16,512]{2,1,0:T(8,128)(2,1)S(1)}, u32[]{:S(2)}, u32[]{:S(2)}) collective-permute-start(bf16[4,16,512]{2,1,0:T(8,128)(2,1)S(1)} %get-tuple-element.48), channel_id=1, source_target_pairs={{0,8},{8,0},{16,24},{24,16},{1,9},{9,1},{17,25},{25,17},{2,10},{10... | collective-permute-start | bytes 196616 | tf_op jit(solution)/shard_map/ppermute | solution.py:624
  31.2 6.8 %collective-permute-start.8 = (bf16[4,16,512]{2,1,0:T(8,128)(2,1)S(1)}, bf16[4,16,512]{2,1,0:T(8,128)(2,1)S(1)}, u32[]{:S(2)}, u32[]{:S(2)}) collective-permute-start(bf16[4,16,512]{2,1,0:T(8,128)(2,1)S(1)} %get-tuple-element.49), channel_id=1, source_target_pairs={{0,24},{8,16},{16,8},{24,0},{1,25},{9,17},{17,9},{25,1},{2,26},{10... | collective-permute-start | bytes 196616 | tf_op jit(solution)/shard_map/ppermute | solution.py:624
  33.6 6.8 %collective-permute-start.7 = (bf16[4,16,512]{2,1,0:T(8,128)(2,1)S(1)}, bf16[4,16,512]{2,1,0:T(8,128)(2,1)S(1)}, u32[]{:S(2)}, u32[]{:S(2)}) collective-permute-start(bf16[4,16,512]{2,1,0:T(8,128)(2,1)S(1)} %get-tuple-element.50), channel_id=1, source_target_pairs={{0,16},{8,24},{16,0},{24,8},{1,17},{9,25},{17,1},{25,9},{2,18},{10... | collective-permute-start | bytes 196616 | tf_op jit(solution)/shard_map/ppermute | solution.py:624
  40.5 5.8 %copy-start = (f32[512,512]{1,0:T(8,128)S(1)}, f32[512,512]{1,0:T(8,128)}, u32[]{:S(2)}) copy-start(f32[512,512]{1,0:T(8,128)} %master.1) | copy-start | bytes 3145732
  40.5 5.8 %copy-start.1 = (f32[512,512]{1,0:T(8,128)S(1)}, f32[512,512]{1,0:T(8,128)}, u32[]{:S(2)}) copy-start(f32[512,512]{1,0:T(8,128)} %first.1) | copy-start | bytes 3145732
  40.6 5.8 %copy-start.2 = (f32[512,512]{1,0:T(8,128)S(1)}, f32[512,512]{1,0:T(8,128)}, u32[]{:S(2)}) copy-start(f32[512,512]{1,0:T(8,128)} %second.1) | copy-start | bytes 3145732
  40.6 18.5 %copy-start.3 = (bf16[4,256,512]{2,1,0:T(8,128)(2,1)S(1)}, bf16[4,256,512]{2,1,0:T(8,128)(2,1)}, u32[]{:S(2)}) copy-start(bf16[4,256,512]{2,1,0:T(8,128)(2,1)} %cache_keys.1) | copy-start | bytes 3145732
  40.6 18.5 %copy-start.4 = (bf16[4,256,512]{2,1,0:T(8,128)(2,1)S(1)}, bf16[4,256,512]{2,1,0:T(8,128)(2,1)}, u32[]{:S(2)}) copy-start(bf16[4,256,512]{2,1,0:T(8,128)(2,1)} %cache_values.1) | copy-start | bytes 3145732
  40.6 18.5 %copy-start.5 = (bf16[4,4,4096]{2,1,0:T(4,128)(2,1)S(1)}, bf16[4,4,4096]{2,1,0:T(4,128)(2,1)}, u32[]{:S(2)}) copy-start(bf16[4,4,4096]{2,1,0:T(4,128)(2,1)} %queries.1) | copy-start | bytes 393220
  40.6 18.5 %copy-start.6 = (bf16[4,4,512]{2,1,0:T(4,128)(2,1)S(1)}, bf16[4,4,512]{2,1,0:T(4,128)(2,1)}, u32[]{:S(2)}) copy-start(bf16[4,4,512]{2,1,0:T(4,128)(2,1)} %new_keys.1) | copy-start | bytes 49156
  40.6 18.5 %copy-start.8 = (s32[4]{0:T(128)S(1)}, s32[4]{0:T(128)}, u32[]{:S(2)}) copy-start(s32[4]{0:T(128)} %lengths.7) | copy-start | bytes 52
  48.4 1.4 %collective-permute-start.9 = (bf16[128,512]{1,0:T(8,128)(2,1)S(1)}, bf16[128,512]{1,0:T(8,128)(2,1)S(1)}, u32[]{:S(2)}, u32[]{:S(2)}) collective-permute-start(bf16[128,512]{1,0:T(8,128)(2,1)S(1)} %get-tuple-element.40), channel_id=1, source_target_pairs={{0,1},{1,0},{2,3},{3,2},{4,5},{5,4},{6,7},{7,6},{8,9},{9,8},{10,11... | collective-permute-start | bytes 393224 | tf_op jit(solution)/shard_map/ppermute | solution.py:640
  49.9 4.7 %collective-permute-start.10 = (bf16[64,512]{1,0:T(8,128)(2,1)S(1)}, bf16[64,512]{1,0:T(8,128)(2,1)S(1)}, u32[]{:S(2)}, u32[]{:S(2)}) collective-permute-start(bf16[64,512]{1,0:T(8,128)(2,1)S(1)} %slice.89), channel_id=1, source_target_pairs={{0,2},{1,3},{2,0},{3,1},{4,6},{5,7},{6,4},{7,5},{8,10},{9,11},{10,... | collective-permute-start | bytes 196616 | tf_op jit(solution)/shard_map/ppermute | solution.py:642
  54.6 7.0 %collective-permute-start.13 = (bf16[16,512]{1,0:T(8,128)(2,1)S(1)}, bf16[16,512]{1,0:T(8,128)(2,1)S(1)}, u32[]{:S(2)}, u32[]{:S(2)}) collective-permute-start(bf16[16,512]{1,0:T(8,128)(2,1)S(1)} %get-tuple-element.55), channel_id=1, source_target_pairs={{0,24},{8,16},{16,8},{24,0},{1,25},{9,17},{17,9},{25,1},{2,26},{10... | collective-permute-start | bytes 49160 | tf_op jit(solution)/shard_map/ppermute | solution.py:647
  57.4 4.6 %collective-permute-start.12 = (bf16[16,512]{1,0:T(8,128)(2,1)S(1)}, bf16[16,512]{1,0:T(8,128)(2,1)S(1)}, u32[]{:S(2)}, u32[]{:S(2)}) collective-permute-start(bf16[16,512]{1,0:T(8,128)(2,1)S(1)} %get-tuple-element.56), channel_id=1, source_target_pairs={{0,16},{8,24},{16,0},{24,8},{1,17},{9,25},{17,1},{25,9},{2,18},{10... | collective-permute-start | bytes 49160 | tf_op jit(solution)/shard_map/ppermute | solution.py:647
  57.4 4.6 %collective-permute-start.11 = (bf16[16,512]{1,0:T(8,128)(2,1)S(1)}, bf16[16,512]{1,0:T(8,128)(2,1)S(1)}, u32[]{:S(2)}, u32[]{:S(2)}) collective-permute-start(bf16[16,512]{1,0:T(8,128)(2,1)S(1)} %get-tuple-element.57), channel_id=1, source_target_pairs={{0,8},{8,0},{16,24},{24,16},{1,9},{9,1},{17,25},{25,17},{2,10},{10... | collective-permute-start | bytes 49160 | tf_op jit(solution)/shard_map/ppermute | solution.py:647
where the time goes:
time: 63.1 us; the launch traced here: 62.9 us
  Pallas kernels  28.7 us (45%)
  starting transfers between devices  17.5 us (28%)
  waiting for transfers between devices  14.7 us (23%)
  between operations  0.91 us (1%)
  local copies, waits for them, and re-layouts  0.8 us (1%)
    pallas_call x1, Pallas kernels, on_device(): pl.pallas_call(functools.partial(first_kernel, span, width, wide_count, r...  11.9 us
    pallas_call x2, Pallas kernels, own_call(): pl.pallas_call(functools.partial(own_kernel, span, width, mine), out_shap...  11.4 us
    ppermute x3, waiting for transfers between devices, on_device(): pieces.append(lax.ppermute(moved[:, dz], 'wide', pairs))  6.67 us
    ppermute x3, starting transfers between devices, on_device(): lax.ppermute(summed[place * lines:(place + 1) * lines].astype(bf16), 'wid...  4.45 us
    ppermute x3, starting transfers between devices, on_device(): pieces.append(lax.ppermute(moved[:, dz], 'wide', pairs))  4.23 us
    ppermute x1, starting transfers between devices, on_device(): lax.ppermute(pieces[3], 'rep', both_pairs)  4 us
    pallas_call x1, Pallas kernels, on_device(): pl.pallas_call(attention_kernel, out_shape=(shape((kv_local, rows, HEAD),...  2.55 us
    ppermute x1, waiting for transfers between devices, on_device(): lax.ppermute(summed[half:].astype(bf16), 'rep', chip_pairs).astype(f32)  2.41 us
  transfers between devices with their start and end apart: 14, of which 8 were waited for; matrix products, arithmetic and copies ran while one was open for 0% of the time, Pallas kernels for 22%

commit v1 on v0

--- a/solution.py
+++ b/solution.py
@@ -137,10 +137,11 @@
     return (new_master, new_first, new_second, new_values, attended)
 
 
-TOKEN_BLOCK = 256
-STEP_BLOCKS = 2
-BUFFERS = 4
-PAD = 4 * STEP_BLOCKS
+TOKEN_BLOCK = 128
+STEP_BLOCKS = 4
+BUFFERS = 5
+TRIP_STEPS = 4
+PAD = TRIP_STEPS * STEP_BLOCKS
 
 
 def live_blocks(lengths, block_of, span, limit_of=None, length_of=None, begin=None):
@@ -159,15 +160,15 @@
             note(count, seq * per_seq + part, length - part * TOKEN_BLOCK, length)
             count = count + jnp.where(length > part * TOKEN_BLOCK, 1, 0)
         if begin is not None and seq % STEP_BLOCKS == STEP_BLOCKS - 1 and seq // STEP_BLOCKS < BUFFERS - 1:
-            begin(jnp.int32(seq // STEP_BLOCKS))
+            begin(seq // STEP_BLOCKS)
     for pad in range(PAD):
         note(count + pad, 0, 0, 1)
-    return lax.div(count + STEP_BLOCKS - 1, STEP_BLOCKS)
-
-
-def start_acts(acts, buf, sem, block_of, step, column, parts):
+    return jnp.maximum(lax.div(count + STEP_BLOCKS - 1, STEP_BLOCKS), TRIP_STEPS)
+
+
+def start_acts(acts, buf, sem, block_of, step, column, parts, skip=0):
     width = buf.shape[1]
-    for part in range(parts):
+    for part in range(skip, parts):
         first = pl.multiple_of(block_of[step * STEP_BLOCKS + part] * TOKEN_BLOCK, TOKEN_BLOCK)
         pltpu.make_async_copy(
             acts.at[pl.ds(first, TOKEN_BLOCK), pl.ds(column, width)],
@@ -190,7 +191,7 @@
     width,
     wide_count,
     rep_count,
-    lengths,
+    lengths_in,
     acts,
     grads,
     hidden,
@@ -199,6 +200,7 @@
     weighted,
     pieces,
     ahead,
+    lengths,
     block_of,
     limit_of,
     length_of,
@@ -212,6 +214,7 @@
     acts_sem,
     grads_sem,
     hidden_sem,
+    lengths_sem,
     ahead_sem,
 ):
     rep = lax.axis_index("rep")
@@ -222,13 +225,24 @@
     next_column = pl.multiple_of((chip * 2 + 1 - core) * width, width)
     step_rows = STEP_BLOCKS * TOKEN_BLOCK
     cols = grads.shape[1]
+    fetch_lengths = pltpu.make_async_copy(lengths_in, lengths, lengths_sem)
+    fetch_lengths.start()
+    for source, buf, sem, begin in ((grads, grads_buf, grads_sem, 0), (acts, acts_buf, acts_sem, column)):
+        pltpu.make_async_copy(
+            source.at[pl.ds(0, TOKEN_BLOCK), pl.ds(begin, buf.shape[2])],
+            buf.at[0, :TOKEN_BLOCK],
+            sem.at[0],
+        ).start()
     fetch = pltpu.make_async_copy(hidden, loaded, hidden_sem)
     fetch.start()
 
-    def start(step):
+    def start(step, skip=0):
         slot = lax.rem(step, BUFFERS)
-        start_acts(grads, grads_buf.at[slot], grads_sem.at[slot], block_of, step, 0, STEP_BLOCKS)
-        start_acts(acts, acts_buf.at[slot], acts_sem.at[slot], block_of, step, column, STEP_BLOCKS)
+        start_acts(grads, grads_buf.at[slot], grads_sem.at[slot], block_of, step, 0, STEP_BLOCKS, skip)
+        start_acts(acts, acts_buf.at[slot], acts_sem.at[slot], block_of, step, column, STEP_BLOCKS, skip)
+
+    def begin_step(step):
+        start(jnp.int32(step), skip=1 if step == 0 else 0)
 
     def turn(step, target):
         slot = lax.rem(step, BUFFERS)
@@ -244,9 +258,11 @@
             place = pl.multiple_of(step * step_rows + part * TOKEN_BLOCK, TOKEN_BLOCK)
             weighted[:, pl.ds(place, TOKEN_BLOCK)] = turned
 
-    steps = live_blocks(lengths, block_of, span, limit_of, length_of, start)
-    start_acts(acts, ahead, ahead_sem, block_of, 0, next_column, 4 * STEP_BLOCKS)
     acc[...] = jnp.zeros_like(acc)
+    fetch_lengths.wait()
+    steps = live_blocks(lengths, block_of, span, limit_of, length_of, begin_step)
+    for early in range(lengths.shape[0] // STEP_BLOCKS, BUFFERS - 1):
+        start(jnp.int32(early))
     fetch.wait()
     count, rows, _ = loaded.shape
     for step in range(count):
@@ -277,6 +293,10 @@
         acc[...] += product(source[...], acts_buf[slot])
 
     def body(pair, carry):
+        @pl.when(pair == 1)
+        def _():
+            start_acts(acts, ahead, ahead_sem, block_of, 0, next_column, 4 * STEP_BLOCKS)
+
         phase(2 * pair, even, odd)
         phase(2 * pair + 1, odd, even)
         return carry
@@ -339,9 +359,9 @@
         def _():
             start(jnp.int32(early))
 
+    acc[...] = product(weighted[:, :trip_rows], loaded[...])
     if not mine:
         start_acts(acts, ahead, ahead_sem, block_of, 0, my_column, 4 * STEP_BLOCKS)
-    acc[...] = product(weighted[:, :trip_rows], loaded[...])
 
     def body(trip, carry):
         @pl.when(trip + slots - 1 < held)
@@ -562,9 +582,10 @@
             shape((4, wide_count, lines, width), bf16),
             pltpu.VMEM((4 * step_rows, width), bf16),
         ),
-        in_specs=[SMEM, HBM, HBM, HBM],
+        in_specs=[HBM, HBM, HBM, HBM],
         out_specs=(VMEM,) * 5,
         scratch_shapes=[
+            pltpu.SMEM(seq_lengths.shape, jnp.int32),
             table,
             table,
             table,
@@ -579,10 +600,11 @@
             sems,
             pltpu.SemaphoreType.DMA,
             pltpu.SemaphoreType.DMA,
+            pltpu.SemaphoreType.DMA,
         ],
         compiler_params=PARAMS,
         name="first_chunk",
-    )(seq_lengths, activations, in_hbm(value_grads), in_hbm(hidden))
+    )(in_hbm(seq_lengths), activations, in_hbm(value_grads), in_hbm(hidden))
     core_part = lax.ppermute(for_core, "rep", core_pairs)
     both_pairs = [(i, i ^ 3) for i in range(rep_count)]
     moved = jnp.stack(
@@ -605,9 +627,9 @@
             out_specs=(VMEM,) * len(out_shape),
             scratch_shapes=[
                 table,
-                pltpu.VMEM((BUFFERS - 1, 4 * step_rows, width), bf16),
+                pltpu.VMEM((3, 4 * step_rows, width), bf16),
                 pltpu.VMEM((cols, width), f32),
-                pltpu.SemaphoreType.DMA((BUFFERS - 1,)),
+                pltpu.SemaphoreType.DMA((3,)),
             ]
             + [pltpu.SemaphoreType.DMA] * (not mine),
             compiler_params=PARAMS,
@@ -692,7 +714,7 @@
         and master.shape[1] % QUANT == 0
         and (value_grads.shape[0] // seq_lengths.shape[0]) % TOKEN_BLOCK == 0
         and lines == 16
-        and seq_lengths.shape[0] >= BUFFERS * STEP_BLOCKS
+        and seq_lengths.shape[0] >= STEP_BLOCKS
     )
     if not fits:
         return on_device_plain(*args)

time: 63.1 us -> 59.7 us (0.946)
  Pallas kernels: 28.7 us -> 26.6 us
  starting transfers between devices: 17.5 us -> 16.7 us
  local copies, waits for them, and re-layouts: 0.8 us -> 0.16 us
    pallas_call x2, Pallas kernels: 11.4 us -> 10.2 us  [own_call(): pl.pallas_call(functools.partial(own_kernel, span, width, mine), out_shap...]
    pallas_call x1, Pallas kernels: 11.9 us -> 11 us  [on_device(): pl.pallas_call(functools.partial(first_kernel, span, width, wide_count, r...]
    unnamed x19, local copies, waits for them, and re-layouts: 0.72 us -> 0.07 us
  transfers between devices with their start and end apart: 14 -> 14, of which waited for: 8 -> 8; matrix products, arithmetic and copies ran while one was open for 0% -> 0% of each run, Pallas kernels for 22% -> 21%
where the time goes in v1:
time: 59.7 us; the launch traced here: 59.5 us
  Pallas kernels  26.6 us (45%)
  starting transfers between devices  16.7 us (28%)
  waiting for transfers between devices  14.8 us (25%)
  between operations  0.93 us (2%)
    pallas_call x1, Pallas kernels, on_device(): pl.pallas_call(functools.partial(first_kernel, span, width, wide_count, r...  11 us
    pallas_call x2, Pallas kernels, own_call(): pl.pallas_call(functools.partial(own_kernel, span, width, mine), out_shap...  10.2 us
    ppermute x3, waiting for transfers between devices, on_device(): pieces.append(lax.ppermute(moved[:, dz], 'wide', pairs))  6.67 us
    ppermute x3, starting transfers between devices, on_device(): lax.ppermute(summed[place * lines:(place + 1) * lines].astype(bf16), 'wid...  4.45 us
    ppermute x3, starting transfers between devices, on_device(): pieces.append(lax.ppermute(moved[:, dz], 'wide', pairs))  4.23 us
    ppermute x1, starting transfers between devices, on_device(): lax.ppermute(pieces[3], 'rep', both_pairs)  3.84 us
    pallas_call x1, Pallas kernels, on_device(): pl.pallas_call(attention_kernel, out_shape=(shape((kv_local, rows, HEAD),...  2.55 us
    ppermute x1, waiting for transfers between devices, on_device(): lax.ppermute(summed[half:].astype(bf16), 'rep', chip_pairs).astype(f32)  2.41 us
  transfers between devices with their start and end apart: 14, of which 8 were waited for; matrix products, arithmetic and copies ran while one was open for 0% of the time, Pallas kernels for 21%

profile of v1, /device:TPU:0, one launch (start us, length us, event | category | flops | bytes accessed | tf_op | source)
XLA Modules:
  0.0 59.5 jit_solution(1894493295548293219)
XLA Ops:
  0.6 11.0 %first_chunk.1 = (f32[512,512]{1,0:T(8,128)S(1)}, bf16[512,512]{1,0:T(8,128)(2,1)S(1)}, bf16[512,8704]{1,0:T(8,128)(2,1)S(1)}, bf16[4,4,16,512]{3,2,1,0:T(8,128)(2,1)S(1)}, bf16[2048,512]{1,0:T(8,128)(2,1)S(1)}) custom-call(s32[8]{0:T(128)} %lengths.4, bf16[8192,2048]{1,0:T(8,128)(2,1)} %acts.5, bf16[8192,512]{1,0:T(8,128)(2,1)} %grads.1, ...), custom_call_target="tpu_custom_call" | custom-call | tf_op jit(solution)/shard_map/first_chunk/pallas_call | solution.py:576
  11.7 0.1 collective-permute-start
  11.8 3.8 %collective-permute-start.5 = (bf16[4,16,512]{2,1,0:T(8,128)(2,1)S(1)}, bf16[4,16,512]{2,1,0:T(8,128)(2,1)S(1)}, u32[]{:S(2)}, u32[]{:S(2)}) collective-permute-start(bf16[4,16,512]{2,1,0:T(8,128)(2,1)S(1)} %get-tuple-element.52), channel_id=1, source_target_pairs={{0,3},{1,2},{2,1},{3,0},{4,7},{5,6},{6,5},{7,4},{8,11},{9,10},{10,... | collective-permute-start | bytes 196616 | tf_op jit(solution)/shard_map/ppermute | solution.py:615
  15.6 0.0 collective-permute-start.4
  15.6 0.5 collective-permute-start.3
  16.1 2.0 %collective-permute-done.5 = bf16[4,16,512]{2,1,0:T(8,128)(2,1)S(1)} collective-permute-done((bf16[4,16,512]{2,1,0:T(8,128)(2,1)S(1)}, bf16[4,16,512]{2,1,0:T(8,128)(2,1)S(1)}, u32[]{:S(2)}, u32[]{:S(2)}) %collective-permute-start.5) | collective-permute-done | bytes 65568 | tf_op jit(solution)/shard_map/ppermute | solution.py:615
  18.1 2.0 %collective-permute-done.3 = bf16[4,16,512]{2,1,0:T(8,128)(2,1)S(1)} collective-permute-done((bf16[4,16,512]{2,1,0:T(8,128)(2,1)S(1)}, bf16[4,16,512]{2,1,0:T(8,128)(2,1)S(1)}, u32[]{:S(2)}, u32[]{:S(2)}) %collective-permute-start.3) | collective-permute-done | bytes 65568 | tf_op jit(solution)/shard_map/ppermute | solution.py:613
  20.2 0.2 add_convert_fusion.order
  20.4 1.3 %collective-permute-start.2 = (bf16[512,512]{1,0:T(8,128)(2,1)S(1)}, bf16[512,512]{1,0:T(8,128)(2,1)S(1)}, u32[]{:S(2)}, u32[]{:S(2)}) collective-permute-start(bf16[512,512]{1,0:T(8,128)(2,1)S(1)} %add_convert_fusion.order), channel_id=1, source_target_pairs={{0,2},{1,3},{2,0},{3,1},{4,6},{5,7},{6,4},{7,5},{8,10},{9,11},{10,... | collective-permute-start | bytes 1572872 | tf_op jit(solution)/shard_map/ppermute | solution.py:620
  21.6 4.9 %near_chunk.1 = (bf16[512,512]{1,0:T(8,128)(2,1)S(1)}, bf16[2048,512]{1,0:T(8,128)(2,1)S(1)}) custom-call(s32[8]{0:T(128)S(1)} %copy-done.7, bf16[8192,2048]{1,0:T(8,128)(2,1)} %acts.5, bf16[512,8704]{1,0:T(8,128)(2,1)S(1)} %get-tuple-element.24.weighted, bf16[2048,512]{1,0:T(8,128)(2,1)S(1)} %get-tuple-element.25.loaded, ...), custom_call_target="tpu_custom_call" | custom-call | tf_op jit(solution)/shard_map/near_chunk/pallas_call | solution.py:623
  26.6 0.1 collective-permute-start.1
  26.7 1.6 %collective-permute-start.6 = (bf16[4,16,512]{2,1,0:T(8,128)(2,1)S(1)}, bf16[4,16,512]{2,1,0:T(8,128)(2,1)S(1)}, u32[]{:S(2)}, u32[]{:S(2)}) collective-permute-start(bf16[4,16,512]{2,1,0:T(8,128)(2,1)S(1)} %get-tuple-element.48), channel_id=1, source_target_pairs={{0,8},{8,0},{16,24},{24,16},{1,9},{9,1},{17,25},{25,17},{2,10},{10... | collective-permute-start | bytes 196616 | tf_op jit(solution)/shard_map/ppermute | solution.py:646
  28.3 2.5 %collective-permute-start.8 = (bf16[4,16,512]{2,1,0:T(8,128)(2,1)S(1)}, bf16[4,16,512]{2,1,0:T(8,128)(2,1)S(1)}, u32[]{:S(2)}, u32[]{:S(2)}) collective-permute-start(bf16[4,16,512]{2,1,0:T(8,128)(2,1)S(1)} %get-tuple-element.49), channel_id=1, source_target_pairs={{0,24},{8,16},{16,8},{24,0},{1,25},{9,17},{17,9},{25,1},{2,26},{10... | collective-permute-start | bytes 196616 | tf_op jit(solution)/shard_map/ppermute | solution.py:646
  30.8 0.1 collective-permute-start.7
  30.9 0.3 collective-permute-done.6
  31.2 3.9 %collective-permute-done.8 = bf16[4,16,512]{2,1,0:T(8,128)(2,1)S(1)} collective-permute-done((bf16[4,16,512]{2,1,0:T(8,128)(2,1)S(1)}, bf16[4,16,512]{2,1,0:T(8,128)(2,1)S(1)}, u32[]{:S(2)}, u32[]{:S(2)}) %collective-permute-start.8) | collective-permute-done | bytes 65568 | tf_op jit(solution)/shard_map/ppermute | solution.py:646
  35.1 2.5 %collective-permute-done.7 = bf16[4,16,512]{2,1,0:T(8,128)(2,1)S(1)} collective-permute-done((bf16[4,16,512]{2,1,0:T(8,128)(2,1)S(1)}, bf16[4,16,512]{2,1,0:T(8,128)(2,1)S(1)}, u32[]{:S(2)}, u32[]{:S(2)}) %collective-permute-start.7) | collective-permute-done | bytes 65568 | tf_op jit(solution)/shard_map/ppermute | solution.py:646
  37.7 0.0 copy-start
  37.7 0.0 copy-start.3
  37.7 0.0 copy-start.4
  37.8 0.0 copy-start.8
  37.8 5.3 %own_chunk.1.own = f32[512,512]{1,0:T(8,128)S(1)} custom-call(s32[8]{0:T(128)S(1)} %copy-done.7, bf16[8192,2048]{1,0:T(8,128)(2,1)} %acts.5, bf16[512,8704]{1,0:T(8,128)(2,1)S(1)} %get-tuple-element.24.weighted, bf16[2048,512]{1,0:T(8,128)(2,1)S(1)} %get-tuple-element.28.loaded, bf16[512,512]{1,0:T(8,128)(2,1)S(1)} %get-tuple-element.29.order), custom_call_target="tpu_custom_call" | custom-call | tf_op jit(solution)/shard_map/own_chunk/pallas_call | solution.py:623
  43.1 2.0 %update.1 = (f32[512,512]{1,0:T(8,128)S(1)}, f32[512,512]{1,0:T(8,128)S(1)}, f32[512,512]{1,0:T(8,128)S(1)}, f32[128,512]{1,0:T(8,128)S(1)}, bf16[128,512]{1,0:T(8,128)(2,1)S(1)}) custom-call(f32[512,512]{1,0:T(8,128)S(1)} %own_chunk.1.own, bf16[512,512]{1,0:T(8,128)(2,1)S(1)} %collective-permute-done.1.from_core, ...), custom_call_target="tpu_custom_call" | custom-call | tf_op jit(solution)/shard_map/update/pallas_call | solution.py:653
  45.2 0.1 collective-permute-start.9
  45.2 1.3 %collective-permute-done.9 = bf16[128,512]{1,0:T(8,128)(2,1)S(1)} collective-permute-done((bf16[128,512]{1,0:T(8,128)(2,1)S(1)}, bf16[128,512]{1,0:T(8,128)(2,1)S(1)}, u32[]{:S(2)}, u32[]{:S(2)}) %collective-permute-start.9) | collective-permute-done | bytes 131104 | tf_op jit(solution)/shard_map/ppermute | solution.py:662
  46.6 2.2 %collective-permute-start.10 = (bf16[64,512]{1,0:T(8,128)(2,1)S(1)}, bf16[64,512]{1,0:T(8,128)(2,1)S(1)}, u32[]{:S(2)}, u32[]{:S(2)}) collective-permute-start(bf16[64,512]{1,0:T(8,128)(2,1)S(1)} %slice.89), channel_id=1, source_target_pairs={{0,2},{1,3},{2,0},{3,1},{4,6},{5,7},{6,4},{7,5},{8,10},{9,11},{10,... | collective-permute-start | bytes 196616 | tf_op jit(solution)/shard_map/ppermute | solution.py:664
  48.9 2.4 %collective-permute-done.10 = bf16[64,512]{1,0:T(8,128)(2,1)S(1)} collective-permute-done((bf16[64,512]{1,0:T(8,128)(2,1)S(1)}, bf16[64,512]{1,0:T(8,128)(2,1)S(1)}, u32[]{:S(2)}, u32[]{:S(2)}) %collective-permute-start.10) | collective-permute-done | bytes 65568 | tf_op jit(solution)/shard_map/ppermute | solution.py:664
  51.3 2.8 %collective-permute-start.13 = (bf16[16,512]{1,0:T(8,128)(2,1)S(1)}, bf16[16,512]{1,0:T(8,128)(2,1)S(1)}, u32[]{:S(2)}, u32[]{:S(2)}) collective-permute-start(bf16[16,512]{1,0:T(8,128)(2,1)S(1)} %get-tuple-element.55), channel_id=1, source_target_pairs={{0,24},{8,16},{16,8},{24,0},{1,25},{9,17},{17,9},{25,1},{2,26},{10... | collective-permute-start | bytes 49160 | tf_op jit(solution)/shard_map/ppermute | solution.py:669
  54.1 1.7 %collective-permute-start.11 = (bf16[16,512]{1,0:T(8,128)(2,1)S(1)}, bf16[16,512]{1,0:T(8,128)(2,1)S(1)}, u32[]{:S(2)}, u32[]{:S(2)}) collective-permute-start(bf16[16,512]{1,0:T(8,128)(2,1)S(1)} %get-tuple-element.57), channel_id=1, source_target_pairs={{0,8},{8,0},{16,24},{24,16},{1,9},{9,1},{17,25},{25,17},{2,10},{10... | collective-permute-start | bytes 49160 | tf_op jit(solution)/shard_map/ppermute | solution.py:669
  55.8 2.5 %cache_attention.1 = (f32[4,128,128]{2,1,0:T(8,128)S(1)}, bf16[4,128,16]{2,1,0:T(8,128)(2,1)S(1)}, f32[512,512]{1,0:T(8,128)}, f32[512,512]{1,0:T(8,128)}, f32[512,512]{1,0:T(8,128)}) custom-call(s32[4]{0:T(128)S(1)} %copy-done.8, bf16[4,4,4096]{2,1,0:T(4,128)(2,1)S(1)} %copy-done.5, bf16[4,4,512]{2,1,0:T(4,128)(2,1)S(1)} %copy-done.6, ...), custom_call_target="tpu_custom_call" | custom-call | tf_op jit(solution)/shard_map/cache_attention/pallas_call | solution.py:673
  58.4 0.3 collective-permute-done.12.refs_4_
  58.7 0.8 %finish.1 = (bf16[4,4,512]{2,1,0:T(4,128)(2,1)}, bf16[4,4,4096]{2,1,0:T(4,128)(2,1)}) custom-call(f32[4,128,128]{2,1,0:T(8,128)S(1)} %get-tuple-element.37.refs_0_, bf16[4,128,16]{2,1,0:T(8,128)(2,1)S(1)} %get-tuple-element.38.refs_1_, f32[16,512]{1,0:T(8,128)S(1)} %slice.76.refs_2_, bf16[16,512]{1,0:T(8,128)(2,1)S(1)} %collective-permute-done.11.refs_3_, ...), custom_call_target="tpu_custom_call" | custom-call | tf_op jit(solution)/shard_map/finish/pallas_call | solution.py:690
  (33 shorter events, 0.3 us)
Async XLA Ops:
  0.6 21.0 %copy-start.7 = (s32[8]{0:T(128)S(1)}, s32[8]{0:T(128)}, u32[]{:S(2)}) copy-start(s32[8]{0:T(128)} %lengths.4) | copy-start | bytes 100
  11.7 8.5 %collective-permute-start = (bf16[512,512]{1,0:T(8,128)(2,1)S(1)}, bf16[512,512]{1,0:T(8,128)(2,1)S(1)}, u32[]{:S(2)}, u32[]{:S(2)}) collective-permute-start(bf16[512,512]{1,0:T(8,128)(2,1)S(1)} %get-tuple-element.27), channel_id=1, source_target_pairs={{0,1},{1,0},{2,3},{3,2},{4,5},{5,4},{6,7},{7,6},{8,9},{9,8},{10,11... | collective-permute-start | bytes 1572872 | tf_op jit(solution)/shard_map/ppermute | solution.py:608
  11.8 6.3 %collective-permute-start.5 = (bf16[4,16,512]{2,1,0:T(8,128)(2,1)S(1)}, bf16[4,16,512]{2,1,0:T(8,128)(2,1)S(1)}, u32[]{:S(2)}, u32[]{:S(2)}) collective-permute-start(bf16[4,16,512]{2,1,0:T(8,128)(2,1)S(1)} %get-tuple-element.52), channel_id=1, source_target_pairs={{0,3},{1,2},{2,1},{3,0},{4,7},{5,6},{6,5},{7,4},{8,11},{9,10},{10,... | collective-permute-start | bytes 196616 | tf_op jit(solution)/shard_map/ppermute | solution.py:615
  15.6 2.5 %collective-permute-start.4 = (bf16[4,16,512]{2,1,0:T(8,128)(2,1)S(1)}, bf16[4,16,512]{2,1,0:T(8,128)(2,1)S(1)}, u32[]{:S(2)}, u32[]{:S(2)}) collective-permute-start(bf16[4,16,512]{2,1,0:T(8,128)(2,1)S(1)} %get-tuple-element.53), channel_id=1, source_target_pairs={{0,1},{1,0},{2,3},{3,2},{4,5},{5,4},{6,7},{7,6},{8,9},{9,8},{10,11... | collective-permute-start | bytes 196616 | tf_op jit(solution)/shard_map/ppermute | solution.py:614
  15.6 4.5 %collective-permute-start.3 = (bf16[4,16,512]{2,1,0:T(8,128)(2,1)S(1)}, bf16[4,16,512]{2,1,0:T(8,128)(2,1)S(1)}, u32[]{:S(2)}, u32[]{:S(2)}) collective-permute-start(bf16[4,16,512]{2,1,0:T(8,128)(2,1)S(1)} %get-tuple-element.54), channel_id=1, source_target_pairs={{0,2},{1,3},{2,0},{3,1},{4,6},{5,7},{6,4},{7,5},{8,10},{9,11},{10,... | collective-permute-start | bytes 196616 | tf_op jit(solution)/shard_map/ppermute | solution.py:613
  20.4 22.7 %collective-permute-start.2 = (bf16[512,512]{1,0:T(8,128)(2,1)S(1)}, bf16[512,512]{1,0:T(8,128)(2,1)S(1)}, u32[]{:S(2)}, u32[]{:S(2)}) collective-permute-start(bf16[512,512]{1,0:T(8,128)(2,1)S(1)} %add_convert_fusion.order), channel_id=1, source_target_pairs={{0,2},{1,3},{2,0},{3,1},{4,6},{5,7},{6,4},{7,5},{8,10},{9,11},{10,... | collective-permute-start | bytes 1572872 | tf_op jit(solution)/shard_map/ppermute | solution.py:620
  26.6 16.5 %collective-permute-start.1 = (bf16[512,512]{1,0:T(8,128)(2,1)S(1)}, bf16[512,512]{1,0:T(8,128)(2,1)S(1)}, u32[]{:S(2)}, u32[]{:S(2)}) collective-permute-start(bf16[512,512]{1,0:T(8,128)(2,1)S(1)} %get-tuple-element.29.order), channel_id=1, source_target_pairs={{0,1},{1,0},{2,3},{3,2},{4,5},{5,4},{6,7},{7,6},{8,9},{9,8},{10,11... | collective-permute-start | bytes 1572872 | tf_op jit(solution)/shard_map/ppermute | solution.py:642
  26.7 4.6 %collective-permute-start.6 = (bf16[4,16,512]{2,1,0:T(8,128)(2,1)S(1)}, bf16[4,16,512]{2,1,0:T(8,128)(2,1)S(1)}, u32[]{:S(2)}, u32[]{:S(2)}) collective-permute-start(bf16[4,16,512]{2,1,0:T(8,128)(2,1)S(1)} %get-tuple-element.48), channel_id=1, source_target_pairs={{0,8},{8,0},{16,24},{24,16},{1,9},{9,1},{17,25},{25,17},{2,10},{10... | collective-permute-start | bytes 196616 | tf_op jit(solution)/shard_map/ppermute | solution.py:646
  28.3 6.8 %collective-permute-start.8 = (bf16[4,16,512]{2,1,0:T(8,128)(2,1)S(1)}, bf16[4,16,512]{2,1,0:T(8,128)(2,1)S(1)}, u32[]{:S(2)}, u32[]{:S(2)}) collective-permute-start(bf16[4,16,512]{2,1,0:T(8,128)(2,1)S(1)} %get-tuple-element.49), channel_id=1, source_target_pairs={{0,24},{8,16},{16,8},{24,0},{1,25},{9,17},{17,9},{25,1},{2,26},{10... | collective-permute-start | bytes 196616 | tf_op jit(solution)/shard_map/ppermute | solution.py:646
  30.8 6.8 %collective-permute-start.7 = (bf16[4,16,512]{2,1,0:T(8,128)(2,1)S(1)}, bf16[4,16,512]{2,1,0:T(8,128)(2,1)S(1)}, u32[]{:S(2)}, u32[]{:S(2)}) collective-permute-start(bf16[4,16,512]{2,1,0:T(8,128)(2,1)S(1)} %get-tuple-element.50), channel_id=1, source_target_pairs={{0,16},{8,24},{16,0},{24,8},{1,17},{9,25},{17,1},{25,9},{2,18},{10... | collective-permute-start | bytes 196616 | tf_op jit(solution)/shard_map/ppermute | solution.py:646
  37.7 5.4 %copy-start = (f32[512,512]{1,0:T(8,128)S(1)}, f32[512,512]{1,0:T(8,128)}, u32[]{:S(2)}) copy-start(f32[512,512]{1,0:T(8,128)} %master.1) | copy-start | bytes 3145732
  37.7 5.4 %copy-start.1 = (f32[512,512]{1,0:T(8,128)S(1)}, f32[512,512]{1,0:T(8,128)}, u32[]{:S(2)}) copy-start(f32[512,512]{1,0:T(8,128)} %first.1) | copy-start | bytes 3145732
  37.7 5.4 %copy-start.2 = (f32[512,512]{1,0:T(8,128)S(1)}, f32[512,512]{1,0:T(8,128)}, u32[]{:S(2)}) copy-start(f32[512,512]{1,0:T(8,128)} %second.1) | copy-start | bytes 3145732
  37.7 18.0 %copy-start.3 = (bf16[4,256,512]{2,1,0:T(8,128)(2,1)S(1)}, bf16[4,256,512]{2,1,0:T(8,128)(2,1)}, u32[]{:S(2)}) copy-start(bf16[4,256,512]{2,1,0:T(8,128)(2,1)} %cache_keys.1) | copy-start | bytes 3145732
  37.7 18.0 %copy-start.4 = (bf16[4,256,512]{2,1,0:T(8,128)(2,1)S(1)}, bf16[4,256,512]{2,1,0:T(8,128)(2,1)}, u32[]{:S(2)}) copy-start(bf16[4,256,512]{2,1,0:T(8,128)(2,1)} %cache_values.1) | copy-start | bytes 3145732
  37.8 18.0 %copy-start.5 = (bf16[4,4,4096]{2,1,0:T(4,128)(2,1)S(1)}, bf16[4,4,4096]{2,1,0:T(4,128)(2,1)}, u32[]{:S(2)}) copy-start(bf16[4,4,4096]{2,1,0:T(4,128)(2,1)} %queries.1) | copy-start | bytes 393220
  37.8 18.0 %copy-start.6 = (bf16[4,4,512]{2,1,0:T(4,128)(2,1)S(1)}, bf16[4,4,512]{2,1,0:T(4,128)(2,1)}, u32[]{:S(2)}) copy-start(bf16[4,4,512]{2,1,0:T(4,128)(2,1)} %new_keys.1) | copy-start | bytes 49156
  37.8 18.0 %copy-start.8 = (s32[4]{0:T(128)S(1)}, s32[4]{0:T(128)}, u32[]{:S(2)}) copy-start(s32[4]{0:T(128)} %lengths.5) | copy-start | bytes 52
  45.2 1.4 %collective-permute-start.9 = (bf16[128,512]{1,0:T(8,128)(2,1)S(1)}, bf16[128,512]{1,0:T(8,128)(2,1)S(1)}, u32[]{:S(2)}, u32[]{:S(2)}) collective-permute-start(bf16[128,512]{1,0:T(8,128)(2,1)S(1)} %get-tuple-element.40), channel_id=1, source_target_pairs={{0,1},{1,0},{2,3},{3,2},{4,5},{5,4},{6,7},{7,6},{8,9},{9,8},{10,11... | collective-permute-start | bytes 393224 | tf_op jit(solution)/shard_map/ppermute | solution.py:662
  46.6 4.6 %collective-permute-start.10 = (bf16[64,512]{1,0:T(8,128)(2,1)S(1)}, bf16[64,512]{1,0:T(8,128)(2,1)S(1)}, u32[]{:S(2)}, u32[]{:S(2)}) collective-permute-start(bf16[64,512]{1,0:T(8,128)(2,1)S(1)} %slice.89), channel_id=1, source_target_pairs={{0,2},{1,3},{2,0},{3,1},{4,6},{5,7},{6,4},{7,5},{8,10},{9,11},{10,... | collective-permute-start | bytes 196616 | tf_op jit(solution)/shard_map/ppermute | solution.py:664
  51.3 7.0 %collective-permute-start.13 = (bf16[16,512]{1,0:T(8,128)(2,1)S(1)}, bf16[16,512]{1,0:T(8,128)(2,1)S(1)}, u32[]{:S(2)}, u32[]{:S(2)}) collective-permute-start(bf16[16,512]{1,0:T(8,128)(2,1)S(1)} %get-tuple-element.55), channel_id=1, source_target_pairs={{0,24},{8,16},{16,8},{24,0},{1,25},{9,17},{17,9},{25,1},{2,26},{10... | collective-permute-start | bytes 49160 | tf_op jit(solution)/shard_map/ppermute | solution.py:669
  54.1 4.6 %collective-permute-start.12 = (bf16[16,512]{1,0:T(8,128)(2,1)S(1)}, bf16[16,512]{1,0:T(8,128)(2,1)S(1)}, u32[]{:S(2)}, u32[]{:S(2)}) collective-permute-start(bf16[16,512]{1,0:T(8,128)(2,1)S(1)} %get-tuple-element.56), channel_id=1, source_target_pairs={{0,16},{8,24},{16,0},{24,8},{1,17},{9,25},{17,1},{25,9},{2,18},{10... | collective-permute-start | bytes 49160 | tf_op jit(solution)/shard_map/ppermute | solution.py:669
  54.1 4.6 %collective-permute-start.11 = (bf16[16,512]{1,0:T(8,128)(2,1)S(1)}, bf16[16,512]{1,0:T(8,128)(2,1)S(1)}, u32[]{:S(2)}, u32[]{:S(2)}) collective-permute-start(bf16[16,512]{1,0:T(8,128)(2,1)S(1)} %get-tuple-element.57), channel_id=1, source_target_pairs={{0,8},{8,0},{16,24},{24,16},{1,9},{9,1},{17,25},{25,17},{2,10},{10... | collective-permute-start | bytes 49160 | tf_op jit(solution)/shard_map/ppermute | solution.py:669

commit v2 on v1

--- a/solution.py
+++ b/solution.py
@@ -139,14 +139,14 @@
 
 TOKEN_BLOCK = 128
 STEP_BLOCKS = 4
-BUFFERS = 5
+BUFFERS = 7
 TRIP_STEPS = 4
 PAD = TRIP_STEPS * STEP_BLOCKS
 
 
-def live_blocks(lengths, block_of, span, limit_of=None, length_of=None, begin=None):
-    count = jnp.int32(0)
+def live_blocks(lengths, block_of, span, limit_of=None, length_of=None):
     per_seq = span // TOKEN_BLOCK
+    seqs = lengths.shape[0]
 
     def note(place, block, limit, length):
         block_of[place] = block
@@ -154,21 +154,22 @@
             limit_of[place] = limit
             length_of[place] = length
 
-    for seq in range(lengths.shape[0]):
+    for seq in range(seqs):
+        note(seq, seq * per_seq, lengths[seq], lengths[seq])
+    count = jnp.int32(seqs)
+    for seq in range(seqs):
         length = lengths[seq]
-        for part in range(per_seq):
+        for part in range(1, per_seq):
             note(count, seq * per_seq + part, length - part * TOKEN_BLOCK, length)
             count = count + jnp.where(length > part * TOKEN_BLOCK, 1, 0)
-        if begin is not None and seq % STEP_BLOCKS == STEP_BLOCKS - 1 and seq // STEP_BLOCKS < BUFFERS - 1:
-            begin(seq // STEP_BLOCKS)
     for pad in range(PAD):
         note(count + pad, 0, 0, 1)
     return jnp.maximum(lax.div(count + STEP_BLOCKS - 1, STEP_BLOCKS), TRIP_STEPS)
 
 
-def start_acts(acts, buf, sem, block_of, step, column, parts, skip=0):
+def start_acts(acts, buf, sem, block_of, step, column, parts):
     width = buf.shape[1]
-    for part in range(skip, parts):
+    for part in range(parts):
         first = pl.multiple_of(block_of[step * STEP_BLOCKS + part] * TOKEN_BLOCK, TOKEN_BLOCK)
         pltpu.make_async_copy(
             acts.at[pl.ds(first, TOKEN_BLOCK), pl.ds(column, width)],
@@ -180,6 +181,24 @@
 def wait_acts(acts, buf, sem):
     rows, cols = buf.shape
     pltpu.make_async_copy(acts.at[pl.ds(0, rows), pl.ds(0, cols)], buf, sem).wait()
+
+
+def start_ahead(acts, ahead, sem, block_of, steps, column):
+    start_acts(acts, ahead.at[0], sem.at[0], block_of, 0, column, TRIP_STEPS * STEP_BLOCKS)
+
+    @pl.when(steps >= 2 * TRIP_STEPS)
+    def _():
+        start_acts(
+            acts, ahead.at[1], sem.at[1], block_of, TRIP_STEPS, column, TRIP_STEPS * STEP_BLOCKS
+        )
+
+
+def wait_ahead(acts, ahead, sem, steps):
+    wait_acts(acts, ahead.at[0], sem.at[0])
+
+    @pl.when(steps >= 2 * TRIP_STEPS)
+    def _():
+        wait_acts(acts, ahead.at[1], sem.at[1])
 
 
 def product(left, right):
@@ -227,22 +246,19 @@
     cols = grads.shape[1]
     fetch_lengths = pltpu.make_async_copy(lengths_in, lengths, lengths_sem)
     fetch_lengths.start()
-    for source, buf, sem, begin in ((grads, grads_buf, grads_sem, 0), (acts, acts_buf, acts_sem, column)):
-        pltpu.make_async_copy(
-            source.at[pl.ds(0, TOKEN_BLOCK), pl.ds(begin, buf.shape[2])],
-            buf.at[0, :TOKEN_BLOCK],
-            sem.at[0],
-        ).start()
+
+    def start(step, blocks=block_of):
+        slot = step % BUFFERS if isinstance(step, int) else lax.rem(step, BUFFERS)
+        start_acts(grads, grads_buf.at[slot], grads_sem.at[slot], blocks, step, 0, STEP_BLOCKS)
+        start_acts(acts, acts_buf.at[slot], acts_sem.at[slot], blocks, step, column, STEP_BLOCKS)
+
+    known = [seq * (span // TOKEN_BLOCK) for seq in range(lengths.shape[0])]
+    known_steps = len(known) // STEP_BLOCKS
+    start(0, known)
     fetch = pltpu.make_async_copy(hidden, loaded, hidden_sem)
     fetch.start()
-
-    def start(step, skip=0):
-        slot = lax.rem(step, BUFFERS)
-        start_acts(grads, grads_buf.at[slot], grads_sem.at[slot], block_of, step, 0, STEP_BLOCKS, skip)
-        start_acts(acts, acts_buf.at[slot], acts_sem.at[slot], block_of, step, column, STEP_BLOCKS, skip)
-
-    def begin_step(step):
-        start(jnp.int32(step), skip=1 if step == 0 else 0)
+    for early in range(1, known_steps):
+        start(early, known)
 
     def turn(step, target):
         slot = lax.rem(step, BUFFERS)
@@ -260,9 +276,12 @@
 
     acc[...] = jnp.zeros_like(acc)
     fetch_lengths.wait()
-    steps = live_blocks(lengths, block_of, span, limit_of, length_of, begin_step)
-    for early in range(lengths.shape[0] // STEP_BLOCKS, BUFFERS - 1):
-        start(jnp.int32(early))
+    steps = live_blocks(lengths, block_of, span, limit_of, length_of)
+    for early in range(known_steps, BUFFERS - 1):
+        @pl.when(early < steps)
+        def _():
+            start(early)
+
     fetch.wait()
     count, rows, _ = loaded.shape
     for step in range(count):
@@ -295,7 +314,7 @@
     def body(pair, carry):
         @pl.when(pair == 1)
         def _():
-            start_acts(acts, ahead, ahead_sem, block_of, 0, next_column, 4 * STEP_BLOCKS)
+            start_ahead(acts, ahead, ahead_sem, block_of, steps, next_column)
 
         phase(2 * pair, even, odd)
         phase(2 * pair + 1, odd, even)
@@ -310,7 +329,7 @@
         acc[...] += product(even[...], acts_buf[slot])
 
     split(acc, core, ours, theirs)
-    wait_acts(acts, ahead, ahead_sem)
+    wait_ahead(acts, ahead, ahead_sem, steps)
 
 
 def split(acc, core, ours, theirs):
@@ -354,14 +373,22 @@
             acts, acts_buf.at[slot], acts_sem.at[slot], block_of, 4 * trip, column, 4 * STEP_BLOCKS
         )
 
-    for early in range(1, slots):
+    @pl.when((trips < 2) & (held > 1))
+    def _():
+        start(jnp.int32(1))
+
+    for early in range(2, slots + 1):
         @pl.when(early < held)
         def _():
             start(jnp.int32(early))
 
-    acc[...] = product(weighted[:, :trip_rows], loaded[...])
+    acc[...] = product(weighted[:, :trip_rows], loaded[0])
     if not mine:
-        start_acts(acts, ahead, ahead_sem, block_of, 0, my_column, 4 * STEP_BLOCKS)
+        start_ahead(acts, ahead, ahead_sem, block_of, steps, my_column)
+
+    @pl.when(trips > 1)
+    def _():
+        acc[...] += product(weighted[:, trip_rows : 2 * trip_rows], loaded[1])
 
     def body(trip, carry):
         @pl.when(trip + slots - 1 < held)
@@ -374,7 +401,7 @@
         acc[...] += product(weighted[:, lanes], acts_buf[slot])
         return carry
 
-    lax.fori_loop(1, trips, body, 0)
+    lax.fori_loop(2, trips, body, 0)
     slot = lax.rem(trips, slots)
     begin = trips * trip_rows
 
@@ -395,7 +422,7 @@
 
     out[...] = acc[...].astype(out.dtype)
     if not mine:
-        wait_acts(acts, ahead, ahead_sem)
+        wait_ahead(acts, ahead, ahead_sem, steps)
 
 
 def update_kernel(
@@ -580,7 +607,7 @@
             shape((cols, width), bf16),
             pltpu.VMEM((cols, tokens + step_rows), bf16),
             shape((4, wide_count, lines, width), bf16),
-            pltpu.VMEM((4 * step_rows, width), bf16),
+            pltpu.VMEM((2, 4 * step_rows, width), bf16),
         ),
         in_specs=[HBM, HBM, HBM, HBM],
         out_specs=(VMEM,) * 5,
@@ -600,7 +627,7 @@
             sems,
             pltpu.SemaphoreType.DMA,
             pltpu.SemaphoreType.DMA,
-            pltpu.SemaphoreType.DMA,
+            pltpu.SemaphoreType.DMA((2,)),
         ],
         compiler_params=PARAMS,
         name="first_chunk",
@@ -631,13 +658,13 @@
                 pltpu.VMEM((cols, width), f32),
                 pltpu.SemaphoreType.DMA((3,)),
             ]
-            + [pltpu.SemaphoreType.DMA] * (not mine),
+            + [pltpu.SemaphoreType.DMA((2,))] * (not mine),
             compiler_params=PARAMS,
             name="own_chunk" if mine else "near_chunk",
         )(seq_lengths, activations, weighted, ahead, order)
 
     for_core, ahead = own_call(
-        False, ahead, for_chip, (shape((cols, width), bf16), pltpu.VMEM((4 * step_rows, width), bf16))
+        False, ahead, for_chip, (shape((cols, width), bf16), pltpu.VMEM((2, 4 * step_rows, width), bf16))
     )
     core_part = lax.ppermute(for_core, "rep", core_pairs)
     pieces = [moved[:, 0]]
@@ -715,6 +742,8 @@
         and (value_grads.shape[0] // seq_lengths.shape[0]) % TOKEN_BLOCK == 0
         and lines == 16
         and seq_lengths.shape[0] >= STEP_BLOCKS
+        and seq_lengths.shape[0] % STEP_BLOCKS == 0
+        and seq_lengths.shape[0] < BUFFERS * STEP_BLOCKS
     )
     if not fits:
         return on_device_plain(*args)

time: 59.7 us -> 58.4 us (0.978)
  Pallas kernels: 26.6 us -> 25.7 us
    pallas_call x2, Pallas kernels: 10.2 us -> 9.44 us  [own_call(): pl.pallas_call(functools.partial(own_kernel, span, width, mine), out_shap...]
where the time goes in v2:
time: 58.4 us; the launch traced here: 58.2 us
  Pallas kernels  25.7 us (44%)
  starting transfers between devices  16.3 us (28%)
  waiting for transfers between devices  14.9 us (26%)
  between operations  0.93 us (2%)
    pallas_call x1, Pallas kernels, on_device(): pl.pallas_call(functools.partial(first_kernel, span, width, wide_count, r...  10.8 us
    pallas_call x2, Pallas kernels, own_call(): pl.pallas_call(functools.partial(own_kernel, span, width, mine), out_shap...  9.44 us
    ppermute x3, waiting for transfers between devices, on_device(): pieces.append(lax.ppermute(moved[:, dz], 'wide', pairs))  6.67 us
    ppermute x3, starting transfers between devices, on_device(): lax.ppermute(summed[place * lines:(place + 1) * lines].astype(bf16), 'wid...  4.45 us
    ppermute x3, starting transfers between devices, on_device(): pieces.append(lax.ppermute(moved[:, dz], 'wide', pairs))  4.24 us
    ppermute x1, starting transfers between devices, on_device(): lax.ppermute(pieces[3], 'rep', both_pairs)  3.84 us
    pallas_call x1, Pallas kernels, on_device(): pl.pallas_call(attention_kernel, out_shape=(shape((kv_local, rows, HEAD),...  2.56 us
    ppermute x1, waiting for transfers between devices, on_device(): lax.ppermute(summed[half:].astype(bf16), 'rep', chip_pairs).astype(f32)  2.46 us
  transfers between devices with their start and end apart: 14, of which 8 were waited for; matrix products, arithmetic and copies ran while one was open for 0% of the time, Pallas kernels for 21%

profile of v2, /device:TPU:0, one launch (start us, length us, event | category | flops | bytes accessed | tf_op | source)
XLA Modules:
  0.0 58.2 jit_solution(1519424296267524438)
XLA Ops:
  0.6 10.8 %first_chunk.1 = (f32[512,512]{1,0:T(8,128)S(1)}, bf16[512,512]{1,0:T(8,128)(2,1)S(1)}, bf16[512,8704]{1,0:T(8,128)(2,1)S(1)}, bf16[4,4,16,512]{3,2,1,0:T(8,128)(2,1)S(1)}, bf16[2,2048,512]{2,1,0:T(8,128)(2,1)S(1)}) custom-call(s32[8]{0:T(128)} %lengths.4, bf16[8192,2048]{1,0:T(8,128)(2,1)} %acts.5, bf16[8192,512]{1,0:T(8,128)(2,1)} %grads.1, ...), custom_call_target="tpu_custom_call" | custom-call | tf_op jit(solution)/shard_map/first_chunk/pallas_call | solution.py:603
  11.5 0.1 collective-permute-start
  11.6 3.8 %collective-permute-start.5 = (bf16[4,16,512]{2,1,0:T(8,128)(2,1)S(1)}, bf16[4,16,512]{2,1,0:T(8,128)(2,1)S(1)}, u32[]{:S(2)}, u32[]{:S(2)}) collective-permute-start(bf16[4,16,512]{2,1,0:T(8,128)(2,1)S(1)} %get-tuple-element.52), channel_id=1, source_target_pairs={{0,3},{1,2},{2,1},{3,0},{4,7},{5,6},{6,5},{7,4},{8,11},{9,10},{10,... | collective-permute-start | bytes 196616 | tf_op jit(solution)/shard_map/ppermute | solution.py:642
  15.4 0.0 collective-permute-start.4
  15.4 0.5 collective-permute-start.3
  15.9 2.0 %collective-permute-done.5 = bf16[4,16,512]{2,1,0:T(8,128)(2,1)S(1)} collective-permute-done((bf16[4,16,512]{2,1,0:T(8,128)(2,1)S(1)}, bf16[4,16,512]{2,1,0:T(8,128)(2,1)S(1)}, u32[]{:S(2)}, u32[]{:S(2)}) %collective-permute-start.5) | collective-permute-done | bytes 65568 | tf_op jit(solution)/shard_map/ppermute | solution.py:642
  17.9 2.0 %collective-permute-done.3 = bf16[4,16,512]{2,1,0:T(8,128)(2,1)S(1)} collective-permute-done((bf16[4,16,512]{2,1,0:T(8,128)(2,1)S(1)}, bf16[4,16,512]{2,1,0:T(8,128)(2,1)S(1)}, u32[]{:S(2)}, u32[]{:S(2)}) %collective-permute-start.3) | collective-permute-done | bytes 65568 | tf_op jit(solution)/shard_map/ppermute | solution.py:640
  20.0 0.2 add_convert_fusion.order
  20.1 1.3 %collective-permute-start.2 = (bf16[512,512]{1,0:T(8,128)(2,1)S(1)}, bf16[512,512]{1,0:T(8,128)(2,1)S(1)}, u32[]{:S(2)}, u32[]{:S(2)}) collective-permute-start(bf16[512,512]{1,0:T(8,128)(2,1)S(1)} %add_convert_fusion.order), channel_id=1, source_target_pairs={{0,2},{1,3},{2,0},{3,1},{4,6},{5,7},{6,4},{7,5},{8,10},{9,11},{10,... | collective-permute-start | bytes 1572872 | tf_op jit(solution)/shard_map/ppermute | solution.py:647
  21.4 4.7 %near_chunk.1 = (bf16[512,512]{1,0:T(8,128)(2,1)S(1)}, bf16[2,2048,512]{2,1,0:T(8,128)(2,1)S(1)}) custom-call(s32[8]{0:T(128)S(1)} %copy-done.7, bf16[8192,2048]{1,0:T(8,128)(2,1)} %acts.5, bf16[512,8704]{1,0:T(8,128)(2,1)S(1)} %get-tuple-element.24.weighted, bf16[2,2048,512]{2,1,0:T(8,128)(2,1)S(1)} %get-tuple-element.25.loaded, ...), custom_call_target="tpu_custom_call" | custom-call | tf_op jit(solution)/shard_map/near_chunk/pallas_call | solution.py:650
  26.0 0.1 collective-permute-start.1
  26.2 1.6 %collective-permute-start.6 = (bf16[4,16,512]{2,1,0:T(8,128)(2,1)S(1)}, bf16[4,16,512]{2,1,0:T(8,128)(2,1)S(1)}, u32[]{:S(2)}, u32[]{:S(2)}) collective-permute-start(bf16[4,16,512]{2,1,0:T(8,128)(2,1)S(1)} %get-tuple-element.48), channel_id=1, source_target_pairs={{0,8},{8,0},{16,24},{24,16},{1,9},{9,1},{17,25},{25,17},{2,10},{10... | collective-permute-start | bytes 196616 | tf_op jit(solution)/shard_map/ppermute | solution.py:673
  27.8 2.5 %collective-permute-start.8 = (bf16[4,16,512]{2,1,0:T(8,128)(2,1)S(1)}, bf16[4,16,512]{2,1,0:T(8,128)(2,1)S(1)}, u32[]{:S(2)}, u32[]{:S(2)}) collective-permute-start(bf16[4,16,512]{2,1,0:T(8,128)(2,1)S(1)} %get-tuple-element.49), channel_id=1, source_target_pairs={{0,24},{8,16},{16,8},{24,0},{1,25},{9,17},{17,9},{25,1},{2,26},{10... | collective-permute-start | bytes 196616 | tf_op jit(solution)/shard_map/ppermute | solution.py:673
  30.3 0.1 collective-permute-start.7
  30.4 0.3 collective-permute-done.6
  30.7 3.9 %collective-permute-done.8 = bf16[4,16,512]{2,1,0:T(8,128)(2,1)S(1)} collective-permute-done((bf16[4,16,512]{2,1,0:T(8,128)(2,1)S(1)}, bf16[4,16,512]{2,1,0:T(8,128)(2,1)S(1)}, u32[]{:S(2)}, u32[]{:S(2)}) %collective-permute-start.8) | collective-permute-done | bytes 65568 | tf_op jit(solution)/shard_map/ppermute | solution.py:673
  34.6 2.5 %collective-permute-done.7 = bf16[4,16,512]{2,1,0:T(8,128)(2,1)S(1)} collective-permute-done((bf16[4,16,512]{2,1,0:T(8,128)(2,1)S(1)}, bf16[4,16,512]{2,1,0:T(8,128)(2,1)S(1)}, u32[]{:S(2)}, u32[]{:S(2)}) %collective-permute-start.7) | collective-permute-done | bytes 65568 | tf_op jit(solution)/shard_map/ppermute | solution.py:673
  37.2 0.0 copy-start
  37.2 0.0 copy-start.3
  37.2 0.0 copy-start.4
  37.3 0.0 copy-start.8
  37.3 4.8 %own_chunk.1.own = f32[512,512]{1,0:T(8,128)S(1)} custom-call(s32[8]{0:T(128)S(1)} %copy-done.7, bf16[8192,2048]{1,0:T(8,128)(2,1)} %acts.5, bf16[512,8704]{1,0:T(8,128)(2,1)S(1)} %get-tuple-element.24.weighted, bf16[2,2048,512]{2,1,0:T(8,128)(2,1)S(1)} %get-tuple-element.28.loaded, bf16[512,512]{1,0:T(8,128)(2,1)S(1)} %get-tuple-element.29.order), custom_call_target="tpu_custom_call" | custom-call | tf_op jit(solution)/shard_map/own_chunk/pallas_call | solution.py:650
  42.1 2.0 %update.1 = (f32[512,512]{1,0:T(8,128)S(1)}, f32[512,512]{1,0:T(8,128)S(1)}, f32[512,512]{1,0:T(8,128)S(1)}, f32[128,512]{1,0:T(8,128)S(1)}, bf16[128,512]{1,0:T(8,128)(2,1)S(1)}) custom-call(f32[512,512]{1,0:T(8,128)S(1)} %own_chunk.1.own, bf16[512,512]{1,0:T(8,128)(2,1)S(1)} %collective-permute-done.1.from_core, ...), custom_call_target="tpu_custom_call" | custom-call | tf_op jit(solution)/shard_map/update/pallas_call | solution.py:680
  44.1 0.1 collective-permute-start.9
  44.2 1.3 %collective-permute-done.9 = bf16[128,512]{1,0:T(8,128)(2,1)S(1)} collective-permute-done((bf16[128,512]{1,0:T(8,128)(2,1)S(1)}, bf16[128,512]{1,0:T(8,128)(2,1)S(1)}, u32[]{:S(2)}, u32[]{:S(2)}) %collective-permute-start.9) | collective-permute-done | bytes 131104 | tf_op jit(solution)/shard_map/ppermute | solution.py:689
  45.6 1.9 %collective-permute-start.10 = (bf16[64,512]{1,0:T(8,128)(2,1)S(1)}, bf16[64,512]{1,0:T(8,128)(2,1)S(1)}, u32[]{:S(2)}, u32[]{:S(2)}) collective-permute-start(bf16[64,512]{1,0:T(8,128)(2,1)S(1)} %slice.89), channel_id=1, source_target_pairs={{0,2},{1,3},{2,0},{3,1},{4,6},{5,7},{6,4},{7,5},{8,10},{9,11},{10,... | collective-permute-start | bytes 196616 | tf_op jit(solution)/shard_map/ppermute | solution.py:691
  47.5 2.5 %collective-permute-done.10 = bf16[64,512]{1,0:T(8,128)(2,1)S(1)} collective-permute-done((bf16[64,512]{1,0:T(8,128)(2,1)S(1)}, bf16[64,512]{1,0:T(8,128)(2,1)S(1)}, u32[]{:S(2)}, u32[]{:S(2)}) %collective-permute-start.10) | collective-permute-done | bytes 65568 | tf_op jit(solution)/shard_map/ppermute | solution.py:691
  50.0 2.8 %collective-permute-start.13 = (bf16[16,512]{1,0:T(8,128)(2,1)S(1)}, bf16[16,512]{1,0:T(8,128)(2,1)S(1)}, u32[]{:S(2)}, u32[]{:S(2)}) collective-permute-start(bf16[16,512]{1,0:T(8,128)(2,1)S(1)} %get-tuple-element.55), channel_id=1, source_target_pairs={{0,24},{8,16},{16,8},{24,0},{1,25},{9,17},{17,9},{25,1},{2,26},{10... | collective-permute-start | bytes 49160 | tf_op jit(solution)/shard_map/ppermute | solution.py:696
  52.7 1.7 %collective-permute-start.11 = (bf16[16,512]{1,0:T(8,128)(2,1)S(1)}, bf16[16,512]{1,0:T(8,128)(2,1)S(1)}, u32[]{:S(2)}, u32[]{:S(2)}) collective-permute-start(bf16[16,512]{1,0:T(8,128)(2,1)S(1)} %get-tuple-element.57), channel_id=1, source_target_pairs={{0,8},{8,0},{16,24},{24,16},{1,9},{9,1},{17,25},{25,17},{2,10},{10... | collective-permute-start | bytes 49160 | tf_op jit(solution)/shard_map/ppermute | solution.py:696
  54.4 2.6 %cache_attention.1 = (f32[4,128,128]{2,1,0:T(8,128)S(1)}, bf16[4,128,16]{2,1,0:T(8,128)(2,1)S(1)}, f32[512,512]{1,0:T(8,128)}, f32[512,512]{1,0:T(8,128)}, f32[512,512]{1,0:T(8,128)}) custom-call(s32[4]{0:T(128)S(1)} %copy-done.8, bf16[4,4,4096]{2,1,0:T(4,128)(2,1)S(1)} %copy-done.5, bf16[4,4,512]{2,1,0:T(4,128)(2,1)S(1)} %copy-done.6, ...), custom_call_target="tpu_custom_call" | custom-call | tf_op jit(solution)/shard_map/cache_attention/pallas_call | solution.py:700
  57.0 0.3 collective-permute-done.12.refs_4_
  57.4 0.8 %finish.1 = (bf16[4,4,512]{2,1,0:T(4,128)(2,1)}, bf16[4,4,4096]{2,1,0:T(4,128)(2,1)}) custom-call(f32[4,128,128]{2,1,0:T(8,128)S(1)} %get-tuple-element.37.refs_0_, bf16[4,128,16]{2,1,0:T(8,128)(2,1)S(1)} %get-tuple-element.38.refs_1_, f32[16,512]{1,0:T(8,128)S(1)} %slice.76.refs_2_, bf16[16,512]{1,0:T(8,128)(2,1)S(1)} %collective-permute-done.11.refs_3_, ...), custom_call_target="tpu_custom_call" | custom-call | tf_op jit(solution)/shard_map/finish/pallas_call | solution.py:717
  (33 shorter events, 0.3 us)
Async XLA Ops:
  0.6 20.8 %copy-start.7 = (s32[8]{0:T(128)S(1)}, s32[8]{0:T(128)}, u32[]{:S(2)}) copy-start(s32[8]{0:T(128)} %lengths.4) | copy-start | bytes 100
  11.5 8.5 %collective-permute-start = (bf16[512,512]{1,0:T(8,128)(2,1)S(1)}, bf16[512,512]{1,0:T(8,128)(2,1)S(1)}, u32[]{:S(2)}, u32[]{:S(2)}) collective-permute-start(bf16[512,512]{1,0:T(8,128)(2,1)S(1)} %get-tuple-element.27), channel_id=1, source_target_pairs={{0,1},{1,0},{2,3},{3,2},{4,5},{5,4},{6,7},{7,6},{8,9},{9,8},{10,11... | collective-permute-start | bytes 1572872 | tf_op jit(solution)/shard_map/ppermute | solution.py:635
  11.6 6.3 %collective-permute-start.5 = (bf16[4,16,512]{2,1,0:T(8,128)(2,1)S(1)}, bf16[4,16,512]{2,1,0:T(8,128)(2,1)S(1)}, u32[]{:S(2)}, u32[]{:S(2)}) collective-permute-start(bf16[4,16,512]{2,1,0:T(8,128)(2,1)S(1)} %get-tuple-element.52), channel_id=1, source_target_pairs={{0,3},{1,2},{2,1},{3,0},{4,7},{5,6},{6,5},{7,4},{8,11},{9,10},{10,... | collective-permute-start | bytes 196616 | tf_op jit(solution)/shard_map/ppermute | solution.py:642
  15.4 2.5 %collective-permute-start.4 = (bf16[4,16,512]{2,1,0:T(8,128)(2,1)S(1)}, bf16[4,16,512]{2,1,0:T(8,128)(2,1)S(1)}, u32[]{:S(2)}, u32[]{:S(2)}) collective-permute-start(bf16[4,16,512]{2,1,0:T(8,128)(2,1)S(1)} %get-tuple-element.53), channel_id=1, source_target_pairs={{0,1},{1,0},{2,3},{3,2},{4,5},{5,4},{6,7},{7,6},{8,9},{9,8},{10,11... | collective-permute-start | bytes 196616 | tf_op jit(solution)/shard_map/ppermute | solution.py:641
  15.4 4.5 %collective-permute-start.3 = (bf16[4,16,512]{2,1,0:T(8,128)(2,1)S(1)}, bf16[4,16,512]{2,1,0:T(8,128)(2,1)S(1)}, u32[]{:S(2)}, u32[]{:S(2)}) collective-permute-start(bf16[4,16,512]{2,1,0:T(8,128)(2,1)S(1)} %get-tuple-element.54), channel_id=1, source_target_pairs={{0,2},{1,3},{2,0},{3,1},{4,6},{5,7},{6,4},{7,5},{8,10},{9,11},{10,... | collective-permute-start | bytes 196616 | tf_op jit(solution)/shard_map/ppermute | solution.py:640
  20.1 22.0 %collective-permute-start.2 = (bf16[512,512]{1,0:T(8,128)(2,1)S(1)}, bf16[512,512]{1,0:T(8,128)(2,1)S(1)}, u32[]{:S(2)}, u32[]{:S(2)}) collective-permute-start(bf16[512,512]{1,0:T(8,128)(2,1)S(1)} %add_convert_fusion.order), channel_id=1, source_target_pairs={{0,2},{1,3},{2,0},{3,1},{4,6},{5,7},{6,4},{7,5},{8,10},{9,11},{10,... | collective-permute-start | bytes 1572872 | tf_op jit(solution)/shard_map/ppermute | solution.py:647
  26.0 16.0 %collective-permute-start.1 = (bf16[512,512]{1,0:T(8,128)(2,1)S(1)}, bf16[512,512]{1,0:T(8,128)(2,1)S(1)}, u32[]{:S(2)}, u32[]{:S(2)}) collective-permute-start(bf16[512,512]{1,0:T(8,128)(2,1)S(1)} %get-tuple-element.29.order), channel_id=1, source_target_pairs={{0,1},{1,0},{2,3},{3,2},{4,5},{5,4},{6,7},{7,6},{8,9},{9,8},{10,11... | collective-permute-start | bytes 1572872 | tf_op jit(solution)/shard_map/ppermute | solution.py:669
  26.2 4.6 %collective-permute-start.6 = (bf16[4,16,512]{2,1,0:T(8,128)(2,1)S(1)}, bf16[4,16,512]{2,1,0:T(8,128)(2,1)S(1)}, u32[]{:S(2)}, u32[]{:S(2)}) collective-permute-start(bf16[4,16,512]{2,1,0:T(8,128)(2,1)S(1)} %get-tuple-element.48), channel_id=1, source_target_pairs={{0,8},{8,0},{16,24},{24,16},{1,9},{9,1},{17,25},{25,17},{2,10},{10... | collective-permute-start | bytes 196616 | tf_op jit(solution)/shard_map/ppermute | solution.py:673
  27.8 6.8 %collective-permute-start.8 = (bf16[4,16,512]{2,1,0:T(8,128)(2,1)S(1)}, bf16[4,16,512]{2,1,0:T(8,128)(2,1)S(1)}, u32[]{:S(2)}, u32[]{:S(2)}) collective-permute-start(bf16[4,16,512]{2,1,0:T(8,128)(2,1)S(1)} %get-tuple-element.49), channel_id=1, source_target_pairs={{0,24},{8,16},{16,8},{24,0},{1,25},{9,17},{17,9},{25,1},{2,26},{10... | collective-permute-start | bytes 196616 | tf_op jit(solution)/shard_map/ppermute | solution.py:673
  30.3 6.8 %collective-permute-start.7 = (bf16[4,16,512]{2,1,0:T(8,128)(2,1)S(1)}, bf16[4,16,512]{2,1,0:T(8,128)(2,1)S(1)}, u32[]{:S(2)}, u32[]{:S(2)}) collective-permute-start(bf16[4,16,512]{2,1,0:T(8,128)(2,1)S(1)} %get-tuple-element.50), channel_id=1, source_target_pairs={{0,16},{8,24},{16,0},{24,8},{1,17},{9,25},{17,1},{25,9},{2,18},{10... | collective-permute-start | bytes 196616 | tf_op jit(solution)/shard_map/ppermute | solution.py:673
  37.2 4.9 %copy-start = (f32[512,512]{1,0:T(8,128)S(1)}, f32[512,512]{1,0:T(8,128)}, u32[]{:S(2)}) copy-start(f32[512,512]{1,0:T(8,128)} %master.1) | copy-start | bytes 3145732
  37.2 4.9 %copy-start.1 = (f32[512,512]{1,0:T(8,128)S(1)}, f32[512,512]{1,0:T(8,128)}, u32[]{:S(2)}) copy-start(f32[512,512]{1,0:T(8,128)} %first.1) | copy-start | bytes 3145732
  37.2 4.9 %copy-start.2 = (f32[512,512]{1,0:T(8,128)S(1)}, f32[512,512]{1,0:T(8,128)}, u32[]{:S(2)}) copy-start(f32[512,512]{1,0:T(8,128)} %second.1) | copy-start | bytes 3145732
  37.2 17.2 %copy-start.3 = (bf16[4,256,512]{2,1,0:T(8,128)(2,1)S(1)}, bf16[4,256,512]{2,1,0:T(8,128)(2,1)}, u32[]{:S(2)}) copy-start(bf16[4,256,512]{2,1,0:T(8,128)(2,1)} %cache_keys.1) | copy-start | bytes 3145732
  37.2 17.2 %copy-start.4 = (bf16[4,256,512]{2,1,0:T(8,128)(2,1)S(1)}, bf16[4,256,512]{2,1,0:T(8,128)(2,1)}, u32[]{:S(2)}) copy-start(bf16[4,256,512]{2,1,0:T(8,128)(2,1)} %cache_values.1) | copy-start | bytes 3145732
  37.2 17.2 %copy-start.5 = (bf16[4,4,4096]{2,1,0:T(4,128)(2,1)S(1)}, bf16[4,4,4096]{2,1,0:T(4,128)(2,1)}, u32[]{:S(2)}) copy-start(bf16[4,4,4096]{2,1,0:T(4,128)(2,1)} %queries.1) | copy-start | bytes 393220
  37.2 17.2 %copy-start.6 = (bf16[4,4,512]{2,1,0:T(4,128)(2,1)S(1)}, bf16[4,4,512]{2,1,0:T(4,128)(2,1)}, u32[]{:S(2)}) copy-start(bf16[4,4,512]{2,1,0:T(4,128)(2,1)} %new_keys.1) | copy-start | bytes 49156
  37.3 17.2 %copy-start.8 = (s32[4]{0:T(128)S(1)}, s32[4]{0:T(128)}, u32[]{:S(2)}) copy-start(s32[4]{0:T(128)} %lengths.5) | copy-start | bytes 52
  44.1 1.4 %collective-permute-start.9 = (bf16[128,512]{1,0:T(8,128)(2,1)S(1)}, bf16[128,512]{1,0:T(8,128)(2,1)S(1)}, u32[]{:S(2)}, u32[]{:S(2)}) collective-permute-start(bf16[128,512]{1,0:T(8,128)(2,1)S(1)} %get-tuple-element.40), channel_id=1, source_target_pairs={{0,1},{1,0},{2,3},{3,2},{4,5},{5,4},{6,7},{7,6},{8,9},{9,8},{10,11... | collective-permute-start | bytes 393224 | tf_op jit(solution)/shard_map/ppermute | solution.py:689
  45.6 4.3 %collective-permute-start.10 = (bf16[64,512]{1,0:T(8,128)(2,1)S(1)}, bf16[64,512]{1,0:T(8,128)(2,1)S(1)}, u32[]{:S(2)}, u32[]{:S(2)}) collective-permute-start(bf16[64,512]{1,0:T(8,128)(2,1)S(1)} %slice.89), channel_id=1, source_target_pairs={{0,2},{1,3},{2,0},{3,1},{4,6},{5,7},{6,4},{7,5},{8,10},{9,11},{10,... | collective-permute-start | bytes 196616 | tf_op jit(solution)/shard_map/ppermute | solution.py:691
  50.0 7.1 %collective-permute-start.13 = (bf16[16,512]{1,0:T(8,128)(2,1)S(1)}, bf16[16,512]{1,0:T(8,128)(2,1)S(1)}, u32[]{:S(2)}, u32[]{:S(2)}) collective-permute-start(bf16[16,512]{1,0:T(8,128)(2,1)S(1)} %get-tuple-element.55), channel_id=1, source_target_pairs={{0,24},{8,16},{16,8},{24,0},{1,25},{9,17},{17,9},{25,1},{2,26},{10... | collective-permute-start | bytes 49160 | tf_op jit(solution)/shard_map/ppermute | solution.py:696
  52.7 4.6 %collective-permute-start.12 = (bf16[16,512]{1,0:T(8,128)(2,1)S(1)}, bf16[16,512]{1,0:T(8,128)(2,1)S(1)}, u32[]{:S(2)}, u32[]{:S(2)}) collective-permute-start(bf16[16,512]{1,0:T(8,128)(2,1)S(1)} %get-tuple-element.56), channel_id=1, source_target_pairs={{0,16},{8,24},{16,0},{24,8},{1,17},{9,25},{17,1},{25,9},{2,18},{10... | collective-permute-start | bytes 49160 | tf_op jit(solution)/shard_map/ppermute | solution.py:696
  52.7 4.6 %collective-permute-start.11 = (bf16[16,512]{1,0:T(8,128)(2,1)S(1)}, bf16[16,512]{1,0:T(8,128)(2,1)S(1)}, u32[]{:S(2)}, u32[]{:S(2)}) collective-permute-start(bf16[16,512]{1,0:T(8,128)(2,1)S(1)} %get-tuple-element.57), channel_id=1, source_target_pairs={{0,8},{8,0},{16,24},{24,16},{1,9},{9,1},{17,25},{25,17},{2,10},{10... | collective-permute-start | bytes 49160 | tf_op jit(solution)/shard_map/ppermute | solution.py:696

commit v3 on v2

--- a/solution.py
+++ b/solution.py
@@ -144,27 +144,20 @@
 PAD = TRIP_STEPS * STEP_BLOCKS
 
 
-def live_blocks(lengths, block_of, span, limit_of=None, length_of=None):
+def live_blocks(lengths, block_of, span):
     per_seq = span // TOKEN_BLOCK
     seqs = lengths.shape[0]
-
-    def note(place, block, limit, length):
-        block_of[place] = block
-        if limit_of is not None:
-            limit_of[place] = limit
-            length_of[place] = length
-
     for seq in range(seqs):
-        note(seq, seq * per_seq, lengths[seq], lengths[seq])
+        block_of[seq] = seq * per_seq
     count = jnp.int32(seqs)
     for seq in range(seqs):
         length = lengths[seq]
         for part in range(1, per_seq):
-            note(count, seq * per_seq + part, length - part * TOKEN_BLOCK, length)
+            block_of[count] = seq * per_seq + part
             count = count + jnp.where(length > part * TOKEN_BLOCK, 1, 0)
     for pad in range(PAD):
-        note(count + pad, 0, 0, 1)
-    return jnp.maximum(lax.div(count + STEP_BLOCKS - 1, STEP_BLOCKS), TRIP_STEPS)
+        block_of[count + pad] = 0
+    return count, jnp.maximum(lax.div(count + STEP_BLOCKS - 1, STEP_BLOCKS), TRIP_STEPS)
 
 
 def start_acts(acts, buf, sem, block_of, step, column, parts):
@@ -221,8 +214,6 @@
     ahead,
     lengths,
     block_of,
-    limit_of,
-    length_of,
     acts_buf,
     grads_buf,
     even,
@@ -252,7 +243,9 @@
         start_acts(grads, grads_buf.at[slot], grads_sem.at[slot], blocks, step, 0, STEP_BLOCKS)
         start_acts(acts, acts_buf.at[slot], acts_sem.at[slot], blocks, step, column, STEP_BLOCKS)
 
-    known = [seq * (span // TOKEN_BLOCK) for seq in range(lengths.shape[0])]
+    per_seq = span // TOKEN_BLOCK
+    per_seq_bits = per_seq.bit_length() - 1
+    known = [seq * per_seq for seq in range(lengths.shape[0])]
     known_steps = len(known) // STEP_BLOCKS
     start(0, known)
     fetch = pltpu.make_async_copy(hidden, loaded, hidden_sem)
@@ -266,9 +259,12 @@
             entry = step * STEP_BLOCKS + part
             rows = slice(part * TOKEN_BLOCK, (part + 1) * TOKEN_BLOCK)
             value = grads_buf[slot, rows, :].astype(jnp.float32)
-            length = jnp.full((1, cols), length_of[entry], jnp.int32).astype(jnp.float32)
+            block = block_of[entry]
+            seq_length = lengths[block >> per_seq_bits]
+            limit = jnp.where(entry < count, seq_length - (block & (per_seq - 1)) * TOKEN_BLOCK, 0)
+            length = jnp.full((1, cols), seq_length, jnp.int32).astype(jnp.float32)
             position = lax.broadcasted_iota(jnp.int32, value.shape, 0)
-            scaled = jnp.where(position < limit_of[entry], value * (1.0 / length), 0.0)
+            scaled = jnp.where(position < limit, value * (1.0 / length), 0.0)
             turned = scaled.astype(jnp.bfloat16).T
             target[:, rows] = turned
             place = pl.multiple_of(step * step_rows + part * TOKEN_BLOCK, TOKEN_BLOCK)
@@ -276,15 +272,15 @@
 
     acc[...] = jnp.zeros_like(acc)
     fetch_lengths.wait()
-    steps = live_blocks(lengths, block_of, span, limit_of, length_of)
+    count, steps = live_blocks(lengths, block_of, span)
     for early in range(known_steps, BUFFERS - 1):
         @pl.when(early < steps)
         def _():
             start(early)
 
     fetch.wait()
-    count, rows, _ = loaded.shape
-    for step in range(count):
+    groups, rows, _ = loaded.shape
+    for step in range(groups):
         flat[step * rows : (step + 1) * rows, :] = loaded[step].astype(jnp.float32)
     for dc in range(2):
         for dx in range(2):
@@ -312,9 +308,18 @@
         acc[...] += product(source[...], acts_buf[slot])
 
     def body(pair, carry):
-        @pl.when(pair == 1)
-        def _():
-            start_ahead(acts, ahead, ahead_sem, block_of, steps, next_column)
+        for trip in range(2):
+            @pl.when((pair == 2 * trip + 1) & (steps >= (trip + 1) * TRIP_STEPS))
+            def _():
+                start_acts(
+                    acts,
+                    ahead.at[trip],
+                    ahead_sem.at[trip],
+                    block_of,
+                    trip * TRIP_STEPS,
+                    next_column,
+                    TRIP_STEPS * STEP_BLOCKS,
+                )
 
         phase(2 * pair, even, odd)
         phase(2 * pair + 1, odd, even)
@@ -359,7 +364,7 @@
     first_column = lax.div(rep, 2) * 2 * width
     my_column = pl.multiple_of(first_column + core * width, width)
     column = my_column if mine else pl.multiple_of(first_column + (1 - core) * width, width)
-    steps = live_blocks(lengths, block_of, span)
+    _, steps = live_blocks(lengths, block_of, span)
     trips = lax.div(steps, 4)
     rest = lax.rem(steps, 4)
     step_rows = STEP_BLOCKS * TOKEN_BLOCK
@@ -614,8 +619,6 @@
         scratch_shapes=[
             pltpu.SMEM(seq_lengths.shape, jnp.int32),
             table,
-            table,
-            table,
             buffers(step_rows, 2 * width),
             buffers(step_rows, cols),
             pltpu.VMEM((cols, step_rows), bf16),
@@ -686,9 +689,11 @@
         compiler_params=PARAMS,
         name="update",
     )(own_part, core_part, chip_part, master, first_moment, second_moment, hidden_kept, hidden_sent)
-    summed = kept + lax.ppermute(sent, "rep", core_pairs).astype(f32)
     half = wide_count * lines
-    summed = summed[:half] + lax.ppermute(summed[half:].astype(bf16), "rep", chip_pairs).astype(f32)
+    from_chip = lax.ppermute(kept[half:].astype(bf16), "rep", chip_pairs)
+    from_both = lax.ppermute(sent[half:], "rep", both_pairs)
+    from_core = lax.ppermute(sent[:half], "rep", core_pairs)
+    summed = kept[:half] + from_core.astype(f32) + from_chip.astype(f32) + from_both.astype(f32)
     arrived = []
     for place in range(1, wide_count):
         pairs = [(i, i ^ place) for i in range(wide_count)]
@@ -741,6 +746,7 @@
         and master.shape[1] % QUANT == 0
         and (value_grads.shape[0] // seq_lengths.shape[0]) % TOKEN_BLOCK == 0
         and lines == 16
+        and (value_grads.shape[0] // seq_lengths.shape[0]) & (value_grads.shape[0] // seq_lengths.shape[0] - 1) == 0
         and seq_lengths.shape[0] >= STEP_BLOCKS
         and seq_lengths.shape[0] % STEP_BLOCKS == 0
         and seq_lengths.shape[0] < BUFFERS * STEP_BLOCKS

time: 58.4 us -> 58.5 us (level)
    ppermute x2 -> x3, starting transfers between devices: 1.94 us -> 2.26 us  [the longest x1 1.87 us: on_device(): from_chip = lax.ppermute(kept[half:].astype(bf16), 'rep', chip_pairs)]
    ppermute x2 -> x3, waiting for transfers between devices: 3.79 us -> 3.52 us  [the longest x1 2.05 us: on_device(): from_chip = lax.ppermute(kept[half:].astype(bf16), 'rep', chip_pairs)]
  transfers between devices with their start and end apart: 14 -> 15, of which waited for: 8 -> 8; matrix products, arithmetic and copies ran while one was open for 0% -> 0% of each run, Pallas kernels for 21% -> 21%
where the time goes in v3:
time: 58.5 us; the launch traced here: 58.3 us
  Pallas kernels  25.7 us (44%)
  starting transfers between devices  16.7 us (29%)
  waiting for transfers between devices  14.6 us (25%)
  between operations  0.93 us (2%)
    pallas_call x1, Pallas kernels, on_device(): pl.pallas_call(functools.partial(first_kernel, span, width, wide_count, r...  10.8 us
    pallas_call x2, Pallas kernels, own_call(): pl.pallas_call(functools.partial(own_kernel, span, width, mine), out_shap...  9.44 us
    ppermute x3, waiting for transfers between devices, on_device(): pieces.append(lax.ppermute(moved[:, dz], 'wide', pairs))  6.67 us
    ppermute x3, starting transfers between devices, on_device(): lax.ppermute(summed[place * lines:(place + 1) * lines].astype(bf16), 'wid...  4.45 us
    ppermute x3, starting transfers between devices, on_device(): pieces.append(lax.ppermute(moved[:, dz], 'wide', pairs))  4.24 us
    ppermute x1, starting transfers between devices, on_device(): lax.ppermute(pieces[3], 'rep', both_pairs)  3.84 us
    pallas_call x1, Pallas kernels, on_device(): pl.pallas_call(attention_kernel, out_shape=(shape((kv_local, rows, HEAD),...  2.57 us
    ppermute x1, waiting for transfers between devices, on_device(): from_chip = lax.ppermute(kept[half:].astype(bf16), 'rep', chip_pairs)  2.05 us
  transfers between devices with their start and end apart: 15, of which 8 were waited for; matrix products, arithmetic and copies ran while one was open for 0% of the time, Pallas kernels for 21%

profile of v3, /device:TPU:0, one launch (start us, length us, event | category | flops | bytes accessed | tf_op | source)
XLA Modules:
  0.0 58.3 jit_solution(8600431108123261241)
XLA Ops:
  0.6 10.8 %first_chunk.1 = (f32[512,512]{1,0:T(8,128)S(1)}, bf16[512,512]{1,0:T(8,128)(2,1)S(1)}, bf16[512,8704]{1,0:T(8,128)(2,1)S(1)}, bf16[4,4,16,512]{3,2,1,0:T(8,128)(2,1)S(1)}, bf16[2,2048,512]{2,1,0:T(8,128)(2,1)S(1)}) custom-call(s32[8]{0:T(128)} %lengths.4, bf16[8192,2048]{1,0:T(8,128)(2,1)} %acts.5, bf16[8192,512]{1,0:T(8,128)(2,1)} %grads.1, ...), custom_call_target="tpu_custom_call" | custom-call | tf_op jit(solution)/shard_map/first_chunk/pallas_call | solution.py:608
  11.5 0.1 collective-permute-start
  11.6 3.8 %collective-permute-start.5 = (bf16[4,16,512]{2,1,0:T(8,128)(2,1)S(1)}, bf16[4,16,512]{2,1,0:T(8,128)(2,1)S(1)}, u32[]{:S(2)}, u32[]{:S(2)}) collective-permute-start(bf16[4,16,512]{2,1,0:T(8,128)(2,1)S(1)} %get-tuple-element.52), channel_id=1, source_target_pairs={{0,3},{1,2},{2,1},{3,0},{4,7},{5,6},{6,5},{7,4},{8,11},{9,10},{10,... | collective-permute-start | bytes 196616 | tf_op jit(solution)/shard_map/ppermute | solution.py:645
  15.4 0.0 collective-permute-start.4
  15.5 0.5 collective-permute-start.3
  15.9 2.0 %collective-permute-done.5 = bf16[4,16,512]{2,1,0:T(8,128)(2,1)S(1)} collective-permute-done((bf16[4,16,512]{2,1,0:T(8,128)(2,1)S(1)}, bf16[4,16,512]{2,1,0:T(8,128)(2,1)S(1)}, u32[]{:S(2)}, u32[]{:S(2)}) %collective-permute-start.5) | collective-permute-done | bytes 65568 | tf_op jit(solution)/shard_map/ppermute | solution.py:645
  17.9 2.0 %collective-permute-done.3 = bf16[4,16,512]{2,1,0:T(8,128)(2,1)S(1)} collective-permute-done((bf16[4,16,512]{2,1,0:T(8,128)(2,1)S(1)}, bf16[4,16,512]{2,1,0:T(8,128)(2,1)S(1)}, u32[]{:S(2)}, u32[]{:S(2)}) %collective-permute-start.3) | collective-permute-done | bytes 65568 | tf_op jit(solution)/shard_map/ppermute | solution.py:643
  20.0 0.2 add_convert_fusion.order
  20.2 1.3 %collective-permute-start.2 = (bf16[512,512]{1,0:T(8,128)(2,1)S(1)}, bf16[512,512]{1,0:T(8,128)(2,1)S(1)}, u32[]{:S(2)}, u32[]{:S(2)}) collective-permute-start(bf16[512,512]{1,0:T(8,128)(2,1)S(1)} %add_convert_fusion.order), channel_id=1, source_target_pairs={{0,2},{1,3},{2,0},{3,1},{4,6},{5,7},{6,4},{7,5},{8,10},{9,11},{10,... | collective-permute-start | bytes 1572872 | tf_op jit(solution)/shard_map/ppermute | solution.py:650
  21.4 4.7 %near_chunk.1 = (bf16[512,512]{1,0:T(8,128)(2,1)S(1)}, bf16[2,2048,512]{2,1,0:T(8,128)(2,1)S(1)}) custom-call(s32[8]{0:T(128)S(1)} %copy-done.7, bf16[8192,2048]{1,0:T(8,128)(2,1)} %acts.5, bf16[512,8704]{1,0:T(8,128)(2,1)S(1)} %get-tuple-element.24.weighted, bf16[2,2048,512]{2,1,0:T(8,128)(2,1)S(1)} %get-tuple-element.25.loaded, ...), custom_call_target="tpu_custom_call" | custom-call | tf_op jit(solution)/shard_map/near_chunk/pallas_call | solution.py:653
  26.1 0.1 collective-permute-start.1
  26.2 1.6 %collective-permute-start.6 = (bf16[4,16,512]{2,1,0:T(8,128)(2,1)S(1)}, bf16[4,16,512]{2,1,0:T(8,128)(2,1)S(1)}, u32[]{:S(2)}, u32[]{:S(2)}) collective-permute-start(bf16[4,16,512]{2,1,0:T(8,128)(2,1)S(1)} %get-tuple-element.48), channel_id=1, source_target_pairs={{0,8},{8,0},{16,24},{24,16},{1,9},{9,1},{17,25},{25,17},{2,10},{10... | collective-permute-start | bytes 196616 | tf_op jit(solution)/shard_map/ppermute | solution.py:676
  27.8 2.5 %collective-permute-start.8 = (bf16[4,16,512]{2,1,0:T(8,128)(2,1)S(1)}, bf16[4,16,512]{2,1,0:T(8,128)(2,1)S(1)}, u32[]{:S(2)}, u32[]{:S(2)}) collective-permute-start(bf16[4,16,512]{2,1,0:T(8,128)(2,1)S(1)} %get-tuple-element.49), channel_id=1, source_target_pairs={{0,24},{8,16},{16,8},{24,0},{1,25},{9,17},{17,9},{25,1},{2,26},{10... | collective-permute-start | bytes 196616 | tf_op jit(solution)/shard_map/ppermute | solution.py:676
  30.3 0.1 collective-permute-start.7
  30.4 0.3 collective-permute-done.6
  30.8 3.9 %collective-permute-done.8 = bf16[4,16,512]{2,1,0:T(8,128)(2,1)S(1)} collective-permute-done((bf16[4,16,512]{2,1,0:T(8,128)(2,1)S(1)}, bf16[4,16,512]{2,1,0:T(8,128)(2,1)S(1)}, u32[]{:S(2)}, u32[]{:S(2)}) %collective-permute-start.8) | collective-permute-done | bytes 65568 | tf_op jit(solution)/shard_map/ppermute | solution.py:676
  34.6 2.5 %collective-permute-done.7 = bf16[4,16,512]{2,1,0:T(8,128)(2,1)S(1)} collective-permute-done((bf16[4,16,512]{2,1,0:T(8,128)(2,1)S(1)}, bf16[4,16,512]{2,1,0:T(8,128)(2,1)S(1)}, u32[]{:S(2)}, u32[]{:S(2)}) %collective-permute-start.7) | collective-permute-done | bytes 65568 | tf_op jit(solution)/shard_map/ppermute | solution.py:676
  37.2 0.0 copy-start
  37.2 0.0 copy-start.3
  37.3 0.0 copy-start.4
  37.3 4.8 %own_chunk.1.own = f32[512,512]{1,0:T(8,128)S(1)} custom-call(s32[8]{0:T(128)S(1)} %copy-done.7, bf16[8192,2048]{1,0:T(8,128)(2,1)} %acts.5, bf16[512,8704]{1,0:T(8,128)(2,1)S(1)} %get-tuple-element.24.weighted, bf16[2,2048,512]{2,1,0:T(8,128)(2,1)S(1)} %get-tuple-element.28.loaded, bf16[512,512]{1,0:T(8,128)(2,1)S(1)} %get-tuple-element.29.order), custom_call_target="tpu_custom_call" | custom-call | tf_op jit(solution)/shard_map/own_chunk/pallas_call | solution.py:653
  42.2 2.0 %update.1 = (f32[512,512]{1,0:T(8,128)S(1)}, f32[512,512]{1,0:T(8,128)S(1)}, f32[512,512]{1,0:T(8,128)S(1)}, f32[128,512]{1,0:T(8,128)S(1)}, bf16[128,512]{1,0:T(8,128)(2,1)S(1)}) custom-call(f32[512,512]{1,0:T(8,128)S(1)} %own_chunk.1.own, bf16[512,512]{1,0:T(8,128)(2,1)S(1)} %collective-permute-done.1.from_core, ...), custom_call_target="tpu_custom_call" | custom-call | tf_op jit(solution)/shard_map/update/pallas_call | solution.py:683
  44.2 1.9 %collective-permute-start.10 = (bf16[64,512]{1,0:T(8,128)(2,1)S(1)}, bf16[64,512]{1,0:T(8,128)(2,1)S(1)}, u32[]{:S(2)}, u32[]{:S(2)}) collective-permute-start(bf16[64,512]{1,0:T(8,128)(2,1)S(1)} %slice.96), channel_id=1, source_target_pairs={{0,2},{1,3},{2,0},{3,1},{4,6},{5,7},{6,4},{7,5},{8,10},{9,11},{10,... | collective-permute-start | bytes 196616 | tf_op jit(solution)/shard_map/ppermute | solution.py:693
  46.1 0.1 collective-permute-start.9
  46.2 0.3 collective-permute-start.11
  46.5 2.0 %collective-permute-done.10 = bf16[64,512]{1,0:T(8,128)(2,1)S(1)} collective-permute-done((bf16[64,512]{1,0:T(8,128)(2,1)S(1)}, bf16[64,512]{1,0:T(8,128)(2,1)S(1)}, u32[]{:S(2)}, u32[]{:S(2)}) %collective-permute-start.10) | collective-permute-done | bytes 65568 | tf_op jit(solution)/shard_map/ppermute | solution.py:693
  48.5 1.5 %collective-permute-done.11 = bf16[64,512]{1,0:T(8,128)(2,1)S(1)} collective-permute-done((bf16[64,512]{1,0:T(8,128)(2,1)S(1)}, bf16[64,512]{1,0:T(8,128)(2,1)S(1)}, u32[]{:S(2)}, u32[]{:S(2)}) %collective-permute-start.11) | collective-permute-done | bytes 65568 | tf_op jit(solution)/shard_map/ppermute | solution.py:694
  50.1 2.8 %collective-permute-start.14 = (bf16[16,512]{1,0:T(8,128)(2,1)S(1)}, bf16[16,512]{1,0:T(8,128)(2,1)S(1)}, u32[]{:S(2)}, u32[]{:S(2)}) collective-permute-start(bf16[16,512]{1,0:T(8,128)(2,1)S(1)} %get-tuple-element.57), channel_id=1, source_target_pairs={{0,24},{8,16},{16,8},{24,0},{1,25},{9,17},{17,9},{25,1},{2,26},{10... | collective-permute-start | bytes 49160 | tf_op jit(solution)/shard_map/ppermute | solution.py:701
  52.8 1.7 %collective-permute-start.12 = (bf16[16,512]{1,0:T(8,128)(2,1)S(1)}, bf16[16,512]{1,0:T(8,128)(2,1)S(1)}, u32[]{:S(2)}, u32[]{:S(2)}) collective-permute-start(bf16[16,512]{1,0:T(8,128)(2,1)S(1)} %get-tuple-element.59), channel_id=1, source_target_pairs={{0,8},{8,0},{16,24},{24,16},{1,9},{9,1},{17,25},{25,17},{2,10},{10... | collective-permute-start | bytes 49160 | tf_op jit(solution)/shard_map/ppermute | solution.py:701
  54.5 2.6 %cache_attention.1 = (f32[4,128,128]{2,1,0:T(8,128)S(1)}, bf16[4,128,16]{2,1,0:T(8,128)(2,1)S(1)}, f32[512,512]{1,0:T(8,128)}, f32[512,512]{1,0:T(8,128)}, f32[512,512]{1,0:T(8,128)}) custom-call(s32[4]{0:T(128)S(1)} %copy-done.8, bf16[4,4,4096]{2,1,0:T(4,128)(2,1)S(1)} %copy-done.5, bf16[4,4,512]{2,1,0:T(4,128)(2,1)S(1)} %copy-done.6, ...), custom_call_target="tpu_custom_call" | custom-call | tf_op jit(solution)/shard_map/cache_attention/pallas_call | solution.py:705
  57.1 0.3 collective-permute-done.13.refs_4_
  57.5 0.8 %finish.1 = (bf16[4,4,512]{2,1,0:T(4,128)(2,1)}, bf16[4,4,4096]{2,1,0:T(4,128)(2,1)}) custom-call(f32[4,128,128]{2,1,0:T(8,128)S(1)} %get-tuple-element.37.refs_0_, bf16[4,128,16]{2,1,0:T(8,128)(2,1)S(1)} %get-tuple-element.38.refs_1_, f32[16,512]{1,0:T(8,128)S(1)} %slice.83.refs_2_, bf16[16,512]{1,0:T(8,128)(2,1)S(1)} %collective-permute-done.12.refs_3_, ...), custom_call_target="tpu_custom_call" | custom-call | tf_op jit(solution)/shard_map/finish/pallas_call | solution.py:722
  (35 shorter events, 0.3 us)
Async XLA Ops:
  0.6 20.8 %copy-start.7 = (s32[8]{0:T(128)S(1)}, s32[8]{0:T(128)}, u32[]{:S(2)}) copy-start(s32[8]{0:T(128)} %lengths.4) | copy-start | bytes 100
  11.5 8.5 %collective-permute-start = (bf16[512,512]{1,0:T(8,128)(2,1)S(1)}, bf16[512,512]{1,0:T(8,128)(2,1)S(1)}, u32[]{:S(2)}, u32[]{:S(2)}) collective-permute-start(bf16[512,512]{1,0:T(8,128)(2,1)S(1)} %get-tuple-element.27), channel_id=1, source_target_pairs={{0,1},{1,0},{2,3},{3,2},{4,5},{5,4},{6,7},{7,6},{8,9},{9,8},{10,11... | collective-permute-start | bytes 1572872 | tf_op jit(solution)/shard_map/ppermute | solution.py:638
  11.6 6.3 %collective-permute-start.5 = (bf16[4,16,512]{2,1,0:T(8,128)(2,1)S(1)}, bf16[4,16,512]{2,1,0:T(8,128)(2,1)S(1)}, u32[]{:S(2)}, u32[]{:S(2)}) collective-permute-start(bf16[4,16,512]{2,1,0:T(8,128)(2,1)S(1)} %get-tuple-element.52), channel_id=1, source_target_pairs={{0,3},{1,2},{2,1},{3,0},{4,7},{5,6},{6,5},{7,4},{8,11},{9,10},{10,... | collective-permute-start | bytes 196616 | tf_op jit(solution)/shard_map/ppermute | solution.py:645
  15.4 2.5 %collective-permute-start.4 = (bf16[4,16,512]{2,1,0:T(8,128)(2,1)S(1)}, bf16[4,16,512]{2,1,0:T(8,128)(2,1)S(1)}, u32[]{:S(2)}, u32[]{:S(2)}) collective-permute-start(bf16[4,16,512]{2,1,0:T(8,128)(2,1)S(1)} %get-tuple-element.53), channel_id=1, source_target_pairs={{0,1},{1,0},{2,3},{3,2},{4,5},{5,4},{6,7},{7,6},{8,9},{9,8},{10,11... | collective-permute-start | bytes 196616 | tf_op jit(solution)/shard_map/ppermute | solution.py:644
  15.5 4.5 %collective-permute-start.3 = (bf16[4,16,512]{2,1,0:T(8,128)(2,1)S(1)}, bf16[4,16,512]{2,1,0:T(8,128)(2,1)S(1)}, u32[]{:S(2)}, u32[]{:S(2)}) collective-permute-start(bf16[4,16,512]{2,1,0:T(8,128)(2,1)S(1)} %get-tuple-element.54), channel_id=1, source_target_pairs={{0,2},{1,3},{2,0},{3,1},{4,6},{5,7},{6,4},{7,5},{8,10},{9,11},{10,... | collective-permute-start | bytes 196616 | tf_op jit(solution)/shard_map/ppermute | solution.py:643
  20.2 22.0 %collective-permute-start.2 = (bf16[512,512]{1,0:T(8,128)(2,1)S(1)}, bf16[512,512]{1,0:T(8,128)(2,1)S(1)}, u32[]{:S(2)}, u32[]{:S(2)}) collective-permute-start(bf16[512,512]{1,0:T(8,128)(2,1)S(1)} %add_convert_fusion.order), channel_id=1, source_target_pairs={{0,2},{1,3},{2,0},{3,1},{4,6},{5,7},{6,4},{7,5},{8,10},{9,11},{10,... | collective-permute-start | bytes 1572872 | tf_op jit(solution)/shard_map/ppermute | solution.py:650
  26.1 16.0 %collective-permute-start.1 = (bf16[512,512]{1,0:T(8,128)(2,1)S(1)}, bf16[512,512]{1,0:T(8,128)(2,1)S(1)}, u32[]{:S(2)}, u32[]{:S(2)}) collective-permute-start(bf16[512,512]{1,0:T(8,128)(2,1)S(1)} %get-tuple-element.29.order), channel_id=1, source_target_pairs={{0,1},{1,0},{2,3},{3,2},{4,5},{5,4},{6,7},{7,6},{8,9},{9,8},{10,11... | collective-permute-start | bytes 1572872 | tf_op jit(solution)/shard_map/ppermute | solution.py:672
  26.2 4.6 %collective-permute-start.6 = (bf16[4,16,512]{2,1,0:T(8,128)(2,1)S(1)}, bf16[4,16,512]{2,1,0:T(8,128)(2,1)S(1)}, u32[]{:S(2)}, u32[]{:S(2)}) collective-permute-start(bf16[4,16,512]{2,1,0:T(8,128)(2,1)S(1)} %get-tuple-element.48), channel_id=1, source_target_pairs={{0,8},{8,0},{16,24},{24,16},{1,9},{9,1},{17,25},{25,17},{2,10},{10... | collective-permute-start | bytes 196616 | tf_op jit(solution)/shard_map/ppermute | solution.py:676
  27.8 6.8 %collective-permute-start.8 = (bf16[4,16,512]{2,1,0:T(8,128)(2,1)S(1)}, bf16[4,16,512]{2,1,0:T(8,128)(2,1)S(1)}, u32[]{:S(2)}, u32[]{:S(2)}) collective-permute-start(bf16[4,16,512]{2,1,0:T(8,128)(2,1)S(1)} %get-tuple-element.49), channel_id=1, source_target_pairs={{0,24},{8,16},{16,8},{24,0},{1,25},{9,17},{17,9},{25,1},{2,26},{10... | collective-permute-start | bytes 196616 | tf_op jit(solution)/shard_map/ppermute | solution.py:676
  30.3 6.8 %collective-permute-start.7 = (bf16[4,16,512]{2,1,0:T(8,128)(2,1)S(1)}, bf16[4,16,512]{2,1,0:T(8,128)(2,1)S(1)}, u32[]{:S(2)}, u32[]{:S(2)}) collective-permute-start(bf16[4,16,512]{2,1,0:T(8,128)(2,1)S(1)} %get-tuple-element.50), channel_id=1, source_target_pairs={{0,16},{8,24},{16,0},{24,8},{1,17},{9,25},{17,1},{25,9},{2,18},{10... | collective-permute-start | bytes 196616 | tf_op jit(solution)/shard_map/ppermute | solution.py:676
  37.2 4.9 %copy-start = (f32[512,512]{1,0:T(8,128)S(1)}, f32[512,512]{1,0:T(8,128)}, u32[]{:S(2)}) copy-start(f32[512,512]{1,0:T(8,128)} %master.1) | copy-start | bytes 3145732
  37.2 4.9 %copy-start.1 = (f32[512,512]{1,0:T(8,128)S(1)}, f32[512,512]{1,0:T(8,128)}, u32[]{:S(2)}) copy-start(f32[512,512]{1,0:T(8,128)} %first.1) | copy-start | bytes 3145732
  37.2 4.9 %copy-start.2 = (f32[512,512]{1,0:T(8,128)S(1)}, f32[512,512]{1,0:T(8,128)}, u32[]{:S(2)}) copy-start(f32[512,512]{1,0:T(8,128)} %second.1) | copy-start | bytes 3145732
  37.2 17.3 %copy-start.3 = (bf16[4,256,512]{2,1,0:T(8,128)(2,1)S(1)}, bf16[4,256,512]{2,1,0:T(8,128)(2,1)}, u32[]{:S(2)}) copy-start(bf16[4,256,512]{2,1,0:T(8,128)(2,1)} %cache_keys.1) | copy-start | bytes 3145732
  37.3 17.3 %copy-start.4 = (bf16[4,256,512]{2,1,0:T(8,128)(2,1)S(1)}, bf16[4,256,512]{2,1,0:T(8,128)(2,1)}, u32[]{:S(2)}) copy-start(bf16[4,256,512]{2,1,0:T(8,128)(2,1)} %cache_values.1) | copy-start | bytes 3145732
  37.3 17.2 %copy-start.5 = (bf16[4,4,4096]{2,1,0:T(4,128)(2,1)S(1)}, bf16[4,4,4096]{2,1,0:T(4,128)(2,1)}, u32[]{:S(2)}) copy-start(bf16[4,4,4096]{2,1,0:T(4,128)(2,1)} %queries.1) | copy-start | bytes 393220
  37.3 17.2 %copy-start.6 = (bf16[4,4,512]{2,1,0:T(4,128)(2,1)S(1)}, bf16[4,4,512]{2,1,0:T(4,128)(2,1)}, u32[]{:S(2)}) copy-start(bf16[4,4,512]{2,1,0:T(4,128)(2,1)} %new_keys.1) | copy-start | bytes 49156
  37.3 17.2 %copy-start.8 = (s32[4]{0:T(128)S(1)}, s32[4]{0:T(128)}, u32[]{:S(2)}) copy-start(s32[4]{0:T(128)} %lengths.5) | copy-start | bytes 52
  44.2 4.3 %collective-permute-start.10 = (bf16[64,512]{1,0:T(8,128)(2,1)S(1)}, bf16[64,512]{1,0:T(8,128)(2,1)S(1)}, u32[]{:S(2)}, u32[]{:S(2)}) collective-permute-start(bf16[64,512]{1,0:T(8,128)(2,1)S(1)} %slice.96), channel_id=1, source_target_pairs={{0,2},{1,3},{2,0},{3,1},{4,6},{5,7},{6,4},{7,5},{8,10},{9,11},{10,... | collective-permute-start | bytes 196616 | tf_op jit(solution)/shard_map/ppermute | solution.py:693
  46.1 2.5 %collective-permute-start.9 = (bf16[64,512]{1,0:T(8,128)(2,1)S(1)}, bf16[64,512]{1,0:T(8,128)(2,1)S(1)}, u32[]{:S(2)}, u32[]{:S(2)}) collective-permute-start(bf16[64,512]{1,0:T(8,128)(2,1)S(1)} %get-tuple-element.55), channel_id=1, source_target_pairs={{0,1},{1,0},{2,3},{3,2},{4,5},{5,4},{6,7},{7,6},{8,9},{9,8},{10,11... | collective-permute-start | bytes 196616 | tf_op jit(solution)/shard_map/ppermute | solution.py:695
  46.2 3.8 %collective-permute-start.11 = (bf16[64,512]{1,0:T(8,128)(2,1)S(1)}, bf16[64,512]{1,0:T(8,128)(2,1)S(1)}, u32[]{:S(2)}, u32[]{:S(2)}) collective-permute-start(bf16[64,512]{1,0:T(8,128)(2,1)S(1)} %get-tuple-element.56), channel_id=1, source_target_pairs={{0,3},{1,2},{2,1},{3,0},{4,7},{5,6},{6,5},{7,4},{8,11},{9,10},{10,... | collective-permute-start | bytes 196616 | tf_op jit(solution)/shard_map/ppermute | solution.py:694
  50.1 7.1 %collective-permute-start.14 = (bf16[16,512]{1,0:T(8,128)(2,1)S(1)}, bf16[16,512]{1,0:T(8,128)(2,1)S(1)}, u32[]{:S(2)}, u32[]{:S(2)}) collective-permute-start(bf16[16,512]{1,0:T(8,128)(2,1)S(1)} %get-tuple-element.57), channel_id=1, source_target_pairs={{0,24},{8,16},{16,8},{24,0},{1,25},{9,17},{17,9},{25,1},{2,26},{10... | collective-permute-start | bytes 49160 | tf_op jit(solution)/shard_map/ppermute | solution.py:701
  52.8 4.6 %collective-permute-start.13 = (bf16[16,512]{1,0:T(8,128)(2,1)S(1)}, bf16[16,512]{1,0:T(8,128)(2,1)S(1)}, u32[]{:S(2)}, u32[]{:S(2)}) collective-permute-start(bf16[16,512]{1,0:T(8,128)(2,1)S(1)} %get-tuple-element.58), channel_id=1, source_target_pairs={{0,16},{8,24},{16,0},{24,8},{1,17},{9,25},{17,1},{25,9},{2,18},{10... | collective-permute-start | bytes 49160 | tf_op jit(solution)/shard_map/ppermute | solution.py:701
  52.8 4.6 %collective-permute-start.12 = (bf16[16,512]{1,0:T(8,128)(2,1)S(1)}, bf16[16,512]{1,0:T(8,128)(2,1)S(1)}, u32[]{:S(2)}, u32[]{:S(2)}) collective-permute-start(bf16[16,512]{1,0:T(8,128)(2,1)S(1)} %get-tuple-element.59), channel_id=1, source_target_pairs={{0,8},{8,0},{16,24},{24,16},{1,9},{9,1},{17,25},{25,17},{2,10},{10... | collective-permute-start | bytes 49160 | tf_op jit(solution)/shard_map/ppermute | solution.py:701
